TPU v7x, 256 devices: a whole 4x4x8 slice. The times are simulated.
256 devices in a mesh: cls: 128 (over y, z, x), rep: 2 (over core).
Axes of the slice: x: 4, y: 4, z: 8, core: 2. Of those that a mesh axis runs over, the one named last changes fastest.
Arguments:
- queries: bfloat16 [2, 256, 768], P('rep', 'cls'), may hold values from -16 to 16
- positives: int32 [2, 256, 4], replicated, may hold values from -1 to 786431, as said below
- label_vectors: bfloat16 [786432, 768], P('cls'), may hold values from -80 to 80
- refresh_slot: int32 [], replicated, may hold values from 0 to 7
- features: bfloat16 [98304, 768], P(('cls', 'rep')), may hold values from -6 to 6
- encoder_weight: bfloat16 [768, 768], replicated, may hold values from -0.21875 to 0.21875
- encoder_gain: float32 [768], replicated, may hold values from 0.1 to 1.9
- free_vectors: bfloat16 [98304, 768], P(('cls', 'rep')), may hold values from -3 to 3
- targets: int32 [98304], replicated, may hold values from 0 to 98303, as said below
Outputs:
- loss: float32 [2, 256], P('rep', 'cls')
- query_grads: bfloat16 [2, 256, 768], P('rep', 'cls')
- refreshed_vectors: bfloat16 [98304, 768], P(('cls', 'rep'))
Inputs may be any that keep to these rules, and one draw needn't show every extreme that they name: `positives`: each row holds 1 to 4 label ids in its first places and -1 in the rest; ids may repeat within a row. `targets`: A permutation. Refreshed row t belongs to owner t // 768. The b-th aligned block of 384 entries names exactly 3 rows of every owner, all in the half b % 2 of that owner's 768 rows.
All inputs are finite; a program needn't handle non-finite values.
Results may differ from a plain program's by a relative error of at most 0.0048.
Values may be sent and summed in bfloat16 or wider, within the bound.
A program may use at most 128 MiB of HBM per device.

v0:
```python
import jax
import jax.numpy as jnp
from jax import lax
from jax.sharding import Mesh
from jax.sharding import PartitionSpec as P

SLOTS = 8
CLS = ("cls_0", "cls_1", "cls_2")
CLS_REP = ("cls_0", "cls_1", "cls_2", "rep")


def from_partner(value, axis, bit):
    mask = 2**bit
    pairs = [(source, source ^ mask) for source in range(lax.axis_size(axis))]
    return lax.ppermute(value, axis, pairs)


def copy_for_each(shard, axis):
    length = lax.axis_size(axis)
    return lax.all_to_all(
        jnp.broadcast_to(shard[None], (length, *shard.shape)), axis, 0, 0, tiled=True
    )


def in_order(pieces, dim):
    dims = list(pieces.shape[1:])
    dims[dim] *= pieces.shape[0]
    return jnp.moveaxis(pieces, 0, dim).reshape(dims)


def whole_of(shard, axes, dim):
    far, near = axes
    pieces = copy_for_each(copy_for_each(shard, far), near)
    return in_order(pieces.swapaxes(0, 1).reshape(-1, *shard.shape), dim)


def taken_together(shard, axis):
    return copy_for_each(shard, axis).max(axis=0)


def over_axes(shard, axes):
    far, near = axes
    nearer = taken_together(shard, near)
    return taken_together(nearer, far)


def taken_together_2(shard, axis):
    everything = copy_for_each(shard, axis)
    return jnp.sum(everything, axis=0)


def one_axis_at_a_time(shard, axes):
    far, near = axes
    nearer = taken_together_2(shard, near)
    return taken_together_2(nearer, far)


def together(arrays, axis):
    ends = [0]
    for a in arrays:
        ends.append(ends[-1] + a.size)
    running = one_axis_at_a_time(jnp.concatenate([a.ravel() for a in arrays]), axis)
    return tuple((running[b:e].reshape(a.shape) for a, b, e in zip(arrays, ends, ends[1:])))


def split_up(shard, dim, length):
    dims = shard.shape
    pieces = shard.reshape(*dims[:dim], length, dims[dim] // length, *dims[dim + 1 :])
    return jnp.moveaxis(pieces, dim, 0)


def sum_at_owner(shard, axis, dim):
    pieces = split_up(shard, dim, lax.axis_size(axis))
    arrived = lax.all_to_all(pieces, axis, split_axis=0, concat_axis=0, tiled=True)
    return arrived.sum(axis=0)


def sum_in_two_steps(shard, axes, dim):
    far, near = axes
    pieces = split_up(shard, dim, lax.axis_size(far))
    nearer = sum_at_owner(pieces, near, dim + 1)
    arrived = lax.all_to_all(nearer, far, split_axis=0, concat_axis=0, tiled=True)
    return arrived.sum(axis=0)


def per_device(
    queries,
    positives,
    label_vectors,
    refresh_slot,
    features,
    encoder_weight,
    encoder_gain,
    free_vectors,
    targets,
):
    cls_count = lax.axis_size(CLS)
    rep_count = lax.axis_size("rep")
    cls_index = lax.axis_index(CLS)
    rep_index = lax.axis_index("rep")
    lab_rows = label_vectors.shape[0]
    feature_width = label_vectors.shape[1]
    slot_rows = lab_rows // SLOTS
    half_rows = slot_rows // rep_count
    per_owner = half_rows // cls_count
    query_rows = queries.shape[1]
    hidden = jnp.dot(features, encoder_weight, preferred_element_type=jnp.float32)
    normed = (
        hidden * lax.rsqrt(jnp.mean(hidden * hidden, axis=1, keepdims=True) + 1e-06) * encoder_gain
    )
    encoded = normed.astype(jnp.bfloat16)
    block_index = cls_index * rep_count + rep_index
    own_targets = lax.dynamic_slice_in_dim(targets, block_index * half_rows, half_rows)
    sending = encoded[jnp.argsort(own_targets)].reshape(cls_count, per_owner, feature_width)
    arrived = lax.all_to_all(sending, CLS, split_axis=0, concat_axis=0, tiled=True)
    by_source = lax.dynamic_index_in_dim(
        targets.reshape(cls_count, rep_count, half_rows), rep_index, 1, keepdims=False
    )
    row_offsets = by_source - (cls_index * slot_rows + rep_index * half_rows)
    kept_rows = (row_offsets >= 0) & (row_offsets < half_rows)
    row_keys = jnp.sort(jnp.where(kept_rows, row_offsets, half_rows), axis=1)[:, :per_owner]
    placed = arrived.reshape(half_rows, feature_width)[jnp.argsort(row_keys.reshape(-1))]
    refreshed = (free_vectors.astype(jnp.float32) + placed.astype(jnp.float32)).astype(jnp.bfloat16)
    partner = from_partner(refreshed, "rep", 0)
    first_half = jnp.where(rep_index == 0, refreshed, partner)
    second_half = jnp.where(rep_index == 0, partner, refreshed)
    fresh_block = jnp.concatenate([first_half, second_half], axis=0)
    current = lax.dynamic_update_slice(
        label_vectors, fresh_block, (refresh_slot * slot_rows, jnp.zeros((), jnp.int32))
    )
    own_queries = queries.reshape(query_rows, feature_width)
    first_label = cls_index * lab_rows
    label_ids = lax.dynamic_index_in_dim(positives, rep_index, 0, keepdims=False)
    logits = lax.dot_general(
        whole_of(own_queries, (("cls_0", "cls_1"), "cls_2"), 0),
        current,
        (((1,), (1,)), ((), ())),
        preferred_element_type=jnp.float32,
    )
    own_offset = cls_index * query_rows
    usable_count = current.shape[0]
    label_offsets = label_ids - first_label
    valid_ids = label_ids >= 0
    present = valid_ids & (label_offsets >= 0) & (label_offsets < usable_count)
    picked = jnp.take_along_axis(logits, jnp.clip(label_offsets, 0, usable_count - 1), axis=1)
    positive_part = jnp.sum(jnp.where(present, picked, 0.0), axis=1)
    local_peak = jnp.max(logits, axis=1)
    local_total = jnp.sum(jnp.exp(logits - local_peak[:, None]), axis=1)
    local_stats = (local_peak, local_total, positive_part)
    maxima = over_axes(local_stats[0], (("cls_0", "cls_1"), "cls_2"))
    exp_totals, positive_sums = together(
        (local_stats[1] * jnp.exp(local_stats[0] - maxima), local_stats[2]),
        (("cls_0", "cls_1"), "cls_2"),
    )
    log_total = maxima + jnp.log(exp_totals)
    id_count = jnp.sum(valid_ids.astype(jnp.float32), axis=1)
    loss_all = log_total - positive_sums / id_count
    inverse_count = 1.0 / id_count
    label_iota = jnp.arange(usable_count, dtype=jnp.int32)[None, :]
    target_mass = jnp.zeros(logits.shape, jnp.float32)
    for column in range(label_ids.shape[1]):
        matches = (label_offsets[:, column : column + 1] == label_iota) & present[
            :, column : column + 1
        ]
        target_mass = target_mass + jnp.where(matches, inverse_count[:, None], 0.0)
    coefficients = (jnp.exp(logits - log_total[:, None]) - target_mass).astype(jnp.bfloat16)
    own_grads = sum_in_two_steps(
        jnp.dot(coefficients, current, preferred_element_type=jnp.float32),
        (("cls_0", "cls_1"), "cls_2"),
        0,
    )
    own_loss = lax.dynamic_slice_in_dim(loss_all, own_offset, query_rows).reshape(1, query_rows)
    return (
        own_loss,
        own_grads.astype(jnp.bfloat16).reshape(1, query_rows, feature_width),
        refreshed,
    )


def solution(mesh):
    torus = Mesh(
        mesh.devices.reshape(4, 8, 4, mesh.shape["rep"]), ("cls_0", "cls_1", "cls_2", "rep")
    )
    placed = (
        P("rep", CLS, None),
        P(),
        P(CLS, None),
        P(),
        P(CLS_REP, None),
        P(),
        P(),
        P(CLS_REP, None),
        P(),
    )
    return jax.shard_map(
        per_device,
        mesh=torus,
        in_specs=placed,
        out_specs=(P("rep", CLS), P("rep", CLS, None), P(CLS_REP, None)),
        check_vma=False,
    )
```

profile of v0, /device:TPU:32, one launch (start us, length us, event | category | flops | bytes accessed | tf_op | source)
XLA Modules:
  0.0 240.9 jit_solution(14369495773253647212)
XLA Ops:
  7.2 8.1 %copy.43 = bf16[6144,768]{1,0:T(8,128)(2,1)} copy(bf16[6144,768]{1,0:T(8,128)(2,1)} %param.11) | data formatting | bytes 18874368
  15.3 3.8 %sort.39 = (s32[384]{0:T(512)}, s32[384]{0:T(512)S(1)}) sort(s32[384]{0:T(512)S(1)} %dynamic_slice.14, s32[384]{0:T(512)S(1)} %iota.11), dimensions={0}, to_apply=%region_1.0 | sort | flops 3456 | bytes 6144 | tf_op jit(solution)/shard_map/jit(argsort)/sort | solution.py:114
  19.2 0.7 multiply_reduce_fusion
  20.1 2.2 gather_fusion
  22.3 1.1 reshape.110
  23.3 15.1 %all-to-all-start = ((bf16[128,3,768]{2,1,0:T(4,128)(2,1)}), bf16[128,3,768]{2,1,0:T(4,128)(2,1)S(1)}, u32[]{:S(2)}, u32[]{:S(2)}) async-start(bf16[128,3,768]{2,1,0:T(4,128)(2,1)} %reshape.110), calls=%async_computation | async-start | bytes 1572864 | tf_op jit(solution)/shard_map/all_to_all | solution.py:115
  39.7 9.7 %sort.43.cloned.1.call-done = s32[128,384]{1,0:T(8,128)} async-done(((s32[128,384]{1,0:T(8,128)}), s32[128,384]{1,0:T(8,128)}) %sort.43.cloned.1.call-update) | async-done | bytes 196624 | tf_op jit(solution)/shard_map/jit(sort)/sort | solution.py:121
  49.4 0.8 slice.50
  50.5 3.8 %sort.41 = (s32[384]{0:T(512)}, s32[384]{0:T(512)S(1)}) sort(s32[384]{0:T(512)S(1)} %reshape.113, s32[384]{0:T(512)S(1)} %iota.12), dimensions={0}, to_apply=%region_3.4 | sort | flops 3456 | bytes 6144 | tf_op jit(solution)/shard_map/jit(argsort)/sort | solution.py:122
  54.2 8.9 %all-to-all-done = bf16[128,3,768]{2,1,0:T(4,128)(2,1)S(1)} async-done(((bf16[128,3,768]{2,1,0:T(4,128)(2,1)}), bf16[128,3,768]{2,1,0:T(4,128)(2,1)S(1)}, u32[]{:S(2)}, u32[]{:S(2)}) %all-to-all-start) | async-done | bytes 589856 | tf_op jit(solution)/shard_map/all_to_all | solution.py:115
  63.8 5.1 %all-to-all-start.1 = ((bf16[32,2,768]{2,1,0:T(2,128)(2,1)}), bf16[32,2,768]{2,1,0:T(2,128)(2,1)}, u32[]{:S(2)}, u32[]{:S(2)}) async-start(bf16[32,2,768]{2,1,0:T(2,128)(2,1)} %broadcast_in_dim.89), calls=%async_computation.1 | async-start | bytes 196608 | tf_op jit(solution)/shard_map/all_to_all | solution.py:20
  69.4 2.2 gather_fusion.1
  72.0 6.4 %all-to-all-done.1 = bf16[32,2,768]{2,1,0:T(2,128)(2,1)} async-done(((bf16[32,2,768]{2,1,0:T(2,128)(2,1)}), bf16[32,2,768]{2,1,0:T(2,128)(2,1)}, u32[]{:S(2)}, u32[]{:S(2)}) %all-to-all-start.1) | async-done | bytes 98336 | tf_op jit(solution)/shard_map/all_to_all | solution.py:20
  78.4 1.8 broadcast_in_dim.90
  80.2 3.6 %all-to-all-start.2 = ((bf16[4,32,2,768]{3,2,1,0:T(2,128)(2,1)}), bf16[4,32,2,768]{3,2,1,0:T(2,128)(2,1)S(1)}, u32[]{:S(2)}, u32[]{:S(2)}) async-start(bf16[4,32,2,768]{3,2,1,0:T(2,128)(2,1)} %broadcast_in_dim.90), calls=%async_computation.2 | async-start | bytes 786432 | tf_op jit(solution)/shard_map/all_to_all | solution.py:20
  84.8 6.2 %all-to-all-done.2 = bf16[4,32,2,768]{3,2,1,0:T(2,128)(2,1)S(1)} async-done(((bf16[4,32,2,768]{3,2,1,0:T(2,128)(2,1)}), bf16[4,32,2,768]{3,2,1,0:T(2,128)(2,1)S(1)}, u32[]{:S(2)}, u32[]{:S(2)}) %all-to-all-start.2) | async-done | bytes 393248 | tf_op jit(solution)/shard_map/all_to_all | solution.py:20
  91.5 1.1 broadcast_select_fusion.1
  92.6 1.1 maximum_dynamic-update-slice_fusion
  93.8 9.0 %fusion.16 = (f32[256]{0:T(256)S(1)}, f32[6144,256]{1,0:T(8,128)}) fusion(bf16[6144,768]{1,0:T(8,128)(2,1)} %maximum_dynamic-update-slice_fusion, bf16[256,768]{1,0:T(8,128)(2,1)S(1)} %reshape_reshape.6), kind=kOutput, calls=%fused_computation.64 | convolution fusion | flops 2417491712 | bytes 16122880 | tf_op jit(solution)/shard_map/dot_general | solution.py:134
  103.4 3.2 %all-to-all-start.3 = ((f32[4,1,256]{2,1,0:T(1,128)}), f32[4,1,256]{2,1,0:T(1,128)S(1)}, u32[]{:S(2)}, u32[]{:S(2)}) async-start(f32[4,1,256]{2,1,0:T(1,128)} %broadcast_in_dim.91), calls=%async_computation.3 | async-start | bytes 8192 | tf_op jit(solution)/shard_map/all_to_all | solution.py:20
  106.6 3.7 %exponential_reduce_fusion = f32[256]{0:T(256)S(1)} fusion(f32[256]{0:T(256)S(1)} %get-tuple-element.27, f32[6144,256]{1,0:T(8,128)} %get-tuple-element.28), kind=kLoop, calls=%fused_computation.8 | loop fusion | flops 3145472 | bytes 6293504 | tf_op jit(solution)/shard_map/reduce_sum | solution.py:148
  110.3 30.7 %gather_fusion.2 = f32[1024]{0:T(1024)S(1)} fusion(f32[256,6144]{0,1:T(8,128)} %bitcast.45, s32[1024]{0:T(1024)S(1)} %reshape.131), kind=kCustom, calls=%fused_computation.2 | custom fusion | bytes 16384 | tf_op jit(solution)/shard_map/jit(take_along_axis)/gather | solution.py:145
  141.8 17.4 %all-to-all-start.4 = ((f32[32,1,256]{2,1,0:T(1,128)}), f32[32,1,256]{2,1,0:T(1,128)S(1)}, u32[]{:S(2)}, u32[]{:S(2)}) async-start(f32[32,1,256]{2,1,0:T(1,128)} %broadcast_in_dim.92), calls=%async_computation.4 | async-start | bytes 65536 | tf_op jit(solution)/shard_map/all_to_all | solution.py:20
  159.4 8.6 %all-to-all-done.4 = f32[32,1,256]{2,1,0:T(1,128)S(1)} async-done(((f32[32,1,256]{2,1,0:T(1,128)}), f32[32,1,256]{2,1,0:T(1,128)S(1)}, u32[]{:S(2)}, u32[]{:S(2)}) %all-to-all-start.4) | async-done | bytes 32800 | tf_op jit(solution)/shard_map/all_to_all | solution.py:20
  168.1 10.3 %all_to_all.49 = f32[4,1,512]{2,1,0:T(1,128)S(1)} all-to-all(f32[4,1,512]{2,1,0:T(1,128)S(1)} %broadcast_in_dim.95), channel_id=1, replica_groups=mesh['cls_0'=4,'cls_1'=8,'cls_2'=4,'rep'=2] {'cls_2'}, dimensions={0} | all-to-all | bytes 16384 | tf_op jit(solution)/shard_map/all_to_all | solution.py:20
  179.1 4.8 %all-to-all-start.6 = ((f32[32,1,512]{2,1,0:T(1,128)}), f32[32,1,512]{2,1,0:T(1,128)S(1)}, u32[]{:S(2)}, u32[]{:S(2)}) async-start(f32[32,1,512]{2,1,0:T(1,128)} %broadcast_in_dim.96), calls=%async_computation.6 | async-start | bytes 131072 | tf_op jit(solution)/shard_map/all_to_all | solution.py:20
  184.6 8.6 %all-to-all-done.6 = f32[32,1,512]{2,1,0:T(1,128)S(1)} async-done(((f32[32,1,512]{2,1,0:T(1,128)}), f32[32,1,512]{2,1,0:T(1,128)S(1)}, u32[]{:S(2)}, u32[]{:S(2)}) %all-to-all-start.6) | async-done | bytes 65568 | tf_op jit(solution)/shard_map/all_to_all | solution.py:20
  193.3 11.3 %fusion.4 = f32[256,768]{1,0:T(8,128)S(1)} fusion(bf16[6144,768]{1,0:T(8,128)(2,1)} %maximum_dynamic-update-slice_fusion, s32[256]{0:T(256)S(1)} %get-tuple-element.10, s32[256]{0:T(256)S(1)} %get-tuple-element.8, s32[256]{0:T(256)S(1)} %get-tuple-element.9, f32[256]{0:T(256)S(1)} %get-tuple-element.24, s32[256]{0:T(256)S(1)} %get-tuple-element.7, ...), kind=kOutput, calls=%fused_computation.13 | convolution fusion | flops 2444230656 | bytes 16522240 | tf_op jit(solution)/shard_map/dot_general | solution.py:168
  205.2 11.9 %all_to_all.50 = f32[4,32,2,768]{3,2,1,0:T(2,128)S(1)} all-to-all(f32[4,32,2,768]{3,2,1,0:T(2,128)S(1)} %bitcast.46), channel_id=1, replica_groups=mesh['cls_0'=4,'cls_1'=8,'cls_2'=4,'rep'=2] {'cls_2'}, dimensions={0} | all-to-all | bytes 1572864 | tf_op jit(solution)/shard_map/all_to_all | solution.py:74
  217.1 1.1 reduce_sum.78
  218.1 4.7 %all-to-all-start.8 = ((f32[32,2,768]{2,1,0:T(2,128)}), f32[32,2,768]{2,1,0:T(2,128)S(1)}, u32[]{:S(2)}, u32[]{:S(2)}) async-start(f32[32,2,768]{2,1,0:T(2,128)} %reduce_sum.78), calls=%async_computation.8 | async-start | bytes 393216 | tf_op jit(solution)/shard_map/all_to_all | solution.py:82
  223.4 10.0 %all-to-all-done.8 = f32[32,2,768]{2,1,0:T(2,128)S(1)} async-done(((f32[32,2,768]{2,1,0:T(2,128)}), f32[32,2,768]{2,1,0:T(2,128)S(1)}, u32[]{:S(2)}, u32[]{:S(2)}) %all-to-all-start.8) | async-done | bytes 196640 | tf_op jit(solution)/shard_map/all_to_all | solution.py:82
  (63 shorter events, 8.8 us)
Async XLA Ops:
  7.2 12.0 %copy-start = (bf16[768,768]{1,0:T(8,128)(2,1)S(1)}, bf16[768,768]{1,0:T(8,128)(2,1)}, u32[]{:S(2)}) copy-start(bf16[768,768]{1,0:T(8,128)(2,1)} %param.14) | copy-start | bytes 3538948
  7.2 8.1 %copy-start.4 = (s32[98304]{0:T(1024)S(1)}, s32[98304]{0:T(1024)}, u32[]{:S(2)}) copy-start(s32[98304]{0:T(1024)} %param.17) | copy-start | bytes 1179652
  7.2 12.0 %copy-start.2 = (bf16[384,768]{1,0:T(8,128)(2,1)S(1)}, bf16[384,768]{1,0:T(8,128)(2,1)}, u32[]{:S(2)}) copy-start(bf16[384,768]{1,0:T(8,128)(2,1)} %param.13) | copy-start | bytes 1769476
  7.2 12.7 %copy-start.5 = (f32[768]{0:T(1024)S(1)}, f32[768]{0:T(1024)}, u32[]{:S(2)}) copy-start(f32[768]{0:T(1024)} %param.15) | copy-start | bytes 9220
  19.9 43.2 %copy-start.6 = (bf16[1,2,768]{2,1,0:T(2,128)(2,1)S(1)}, bf16[1,2,768]{2,1,0:T(2,128)(2,1)}, u32[]{:S(2)}) copy-start(bf16[1,2,768]{2,1,0:T(2,128)(2,1)} %param.9) | copy-start | bytes 9220
  22.2 49.3 %copy-start.3 = (bf16[384,768]{1,0:T(8,128)(2,1)S(1)}, bf16[384,768]{1,0:T(8,128)(2,1)}, u32[]{:S(2)}) copy-start(bf16[384,768]{1,0:T(8,128)(2,1)} %param.16) | copy-start | bytes 1769476
  23.3 48.5 %copy-start.7 = (s32[2,256,4]{1,2,0:T(4,128)S(1)}, s32[2,256,4]{1,2,0:T(4,128)}, u32[]{:S(2)}) copy-start(s32[2,256,4]{1,2,0:T(4,128)} %param.10) | copy-start | bytes 24580
  23.3 39.8 %all-to-all-start = ((bf16[128,3,768]{2,1,0:T(4,128)(2,1)}), bf16[128,3,768]{2,1,0:T(4,128)(2,1)S(1)}, u32[]{:S(2)}, u32[]{:S(2)}) async-start(bf16[128,3,768]{2,1,0:T(4,128)(2,1)} %reshape.110), calls=%async_computation | async-start | bytes 1572864 | tf_op jit(solution)/shard_map/all_to_all | solution.py:115
  38.5 10.9 %sort.43.cloned.1.call-start = ((), (), s32[]{:S(2)}) async-start(), calls=%async_computation.9 | async-start | bytes 589856 | tf_op jit(solution)/shard_map/jit(sort)/sort | solution.py:121
  63.8 14.6 %all-to-all-start.1 = ((bf16[32,2,768]{2,1,0:T(2,128)(2,1)}), bf16[32,2,768]{2,1,0:T(2,128)(2,1)}, u32[]{:S(2)}, u32[]{:S(2)}) async-start(bf16[32,2,768]{2,1,0:T(2,128)(2,1)} %broadcast_in_dim.89), calls=%async_computation.1 | async-start | bytes 196608 | tf_op jit(solution)/shard_map/all_to_all | solution.py:20
  71.7 31.1 %copy-start.1 = (bf16[384,768]{1,0:T(8,128)(2,1)}, bf16[384,768]{1,0:T(8,128)(2,1)S(1)}, u32[]{:S(2)}) copy-start(bf16[384,768]{1,0:T(8,128)(2,1)S(1)} %add_convert_fusion) | copy-start | bytes 1769476
  71.8 19.7 %collective-permute-start = (bf16[384,768]{1,0:T(8,128)(2,1)S(1)}, bf16[384,768]{1,0:T(8,128)(2,1)}, u32[]{:S(2)}, u32[]{:S(2)}) collective-permute-start(bf16[384,768]{1,0:T(8,128)(2,1)S(1)} %add_convert_fusion), channel_id=1, source_target_pairs={{0,1},{1,0},{2,3},{3,2},{4,5},{5,4},{6,7},{7,6},{8,9},{9,8},{10,11... | collective-permute-start | bytes 1769480 | tf_op jit(solution)/shard_map/ppermute | solution.py:15
  80.2 10.8 %all-to-all-start.2 = ((bf16[4,32,2,768]{3,2,1,0:T(2,128)(2,1)}), bf16[4,32,2,768]{3,2,1,0:T(2,128)(2,1)S(1)}, u32[]{:S(2)}, u32[]{:S(2)}) async-start(bf16[4,32,2,768]{3,2,1,0:T(2,128)(2,1)} %broadcast_in_dim.90), calls=%async_computation.2 | async-start | bytes 786432 | tf_op jit(solution)/shard_map/all_to_all | solution.py:20
  103.4 37.7 %all-to-all-start.3 = ((f32[4,1,256]{2,1,0:T(1,128)}), f32[4,1,256]{2,1,0:T(1,128)S(1)}, u32[]{:S(2)}, u32[]{:S(2)}) async-start(f32[4,1,256]{2,1,0:T(1,128)} %broadcast_in_dim.91), calls=%async_computation.3 | async-start | bytes 8192 | tf_op jit(solution)/shard_map/all_to_all | solution.py:20
  141.8 26.2 %all-to-all-start.4 = ((f32[32,1,256]{2,1,0:T(1,128)}), f32[32,1,256]{2,1,0:T(1,128)S(1)}, u32[]{:S(2)}, u32[]{:S(2)}) async-start(f32[32,1,256]{2,1,0:T(1,128)} %broadcast_in_dim.92), calls=%async_computation.4 | async-start | bytes 65536 | tf_op jit(solution)/shard_map/all_to_all | solution.py:20
  179.1 14.1 %all-to-all-start.6 = ((f32[32,1,512]{2,1,0:T(1,128)}), f32[32,1,512]{2,1,0:T(1,128)S(1)}, u32[]{:S(2)}, u32[]{:S(2)}) async-start(f32[32,1,512]{2,1,0:T(1,128)} %broadcast_in_dim.96), calls=%async_computation.6 | async-start | bytes 131072 | tf_op jit(solution)/shard_map/all_to_all | solution.py:20
  218.1 15.3 %all-to-all-start.8 = ((f32[32,2,768]{2,1,0:T(2,128)}), f32[32,2,768]{2,1,0:T(2,128)S(1)}, u32[]{:S(2)}, u32[]{:S(2)}) async-start(f32[32,2,768]{2,1,0:T(2,128)} %reduce_sum.78), calls=%async_computation.8 | async-start | bytes 393216 | tf_op jit(solution)/shard_map/all_to_all | solution.py:82
Sparse Core Ops, SparseCore 0:
  42.2 6.8 sort.45.cloned.1.call-done
  (1 shorter events, 0.0 us)
where the time goes:
time: 243 us; the launch traced here: 241 us
  local copies, waits for them, and re-layouts  62.9 us (26%)
  starting transfers between devices  54 us (22%)
  waiting for transfers between devices  48.7 us (20%)
  blocking collectives  22.2 us (9%)
  matrix products  21.1 us (9%)
  other arithmetic  17 us (7%)
  between operations  15.1 us (6%)
    all_to_all x5, starting transfers between devices, copy_for_each(): lax.all_to_all(jnp.broadcast_to(shard[None], (length, *shard.shape)), axi...  34.1 us
    gather x3, local copies, waits for them, and re-layouts, per_device(): jnp.take_along_axis(logits, jnp.clip(label_offsets, 0, usable_count - 1),...  30.9 us
    all_to_all x5, waiting for transfers between devices, copy_for_each(): lax.all_to_all(jnp.broadcast_to(shard[None], (length, *shard.shape)), axi...  29.8 us
    all_to_all x1, starting transfers between devices, per_device(): lax.all_to_all(sending, CLS, split_axis=0, concat_axis=0, tiled=True)  15.1 us
    all_to_all x1, blocking collectives, sum_at_owner(): lax.all_to_all(pieces, axis, split_axis=0, concat_axis=0, tiled=True)  11.9 us
    dot_general x1, matrix products, per_device(): jnp.dot(coefficients, current, preferred_element_type=jnp.float32)  11.3 us
    all_to_all x1, blocking collectives, copy_for_each(): lax.all_to_all(jnp.broadcast_to(shard[None], (length, *shard.shape)), axi...  10.3 us
    all_to_all x1, waiting for transfers between devices, sum_in_two_steps(): lax.all_to_all(nearer, far, split_axis=0, concat_axis=0, tiled=True)  10 us
  transfers between devices with their start and end apart: 8, of which 6 were waited for; matrix products, arithmetic and copies ran while one was open for 20% of the time, Pallas kernels for 0%

commit v1 on v0

v1 whole, which is shorter than its diff:
```python
import jax
import jax.numpy as jnp
from jax import lax
from jax.experimental import pallas as pl
from jax.experimental.pallas import tpu as pltpu
from jax.sharding import Mesh
from jax.sharding import PartitionSpec as P

F32 = jnp.float32
BF16 = jnp.bfloat16
I32 = jnp.int32
MESH = pl.DeviceIdType.MESH
CLS = ("y", "z", "x")
CLS_REP = ("y", "z", "x", "core")
NY, NZ, NX = 4, 8, 4
NPLANE = NX * NY
NCLS = NPLANE * NZ
D = 768
HALF = D // 2
ROWS = 384
SLOTS = 8
SLOT_ROWS = 768
LABELS_DEV = SLOTS * SLOT_ROWS
NQ = 256
POS = 4
CHUNK = 32
LANES = 128
TILES = SLOT_ROWS // LANES


def dot(a, b):
    return jnp.dot(a, b, preferred_element_type=F32)


def dot_t(a, b):
    return lax.dot_general(a, b, (((1,), (1,)), ((), ())), preferred_element_type=F32)


def each(lo, hi, fn):
    def step(k, carry):
        fn(k)
        return carry

    lax.fori_loop(lo, hi, step, 0)


def three_of(parts, inside):
    low = high = total = None
    for part, mask in zip(parts, inside):
        lo = jnp.min(jnp.where(mask, part, 1e9), axis=1, keepdims=True)
        hi = jnp.max(jnp.where(mask, part, -1.0), axis=1, keepdims=True)
        su = jnp.sum(jnp.where(mask, part, 0.0), axis=1, keepdims=True)
        low = lo if low is None else jnp.minimum(low, lo)
        high = hi if high is None else jnp.maximum(high, hi)
        total = su if total is None else total + su
    return low, total - low - high, high


def merged(stats, count):
    peak = stats[0, 0:1, :]
    for i in range(1, count):
        peak = jnp.maximum(peak, stats[i, 0:1, :])
    total = jnp.zeros_like(peak)
    positive = jnp.zeros_like(peak)
    for i in range(count):
        total = total + stats[i, 1:2, :] * jnp.exp(stats[i, 0:1, :] - peak)
        positive = positive + stats[i, 2:3, :]
    return peak, total, positive


def kernel(
    slot_ref, q_hbm, pos_ref, lab_hbm, feat_ref, w_ref, gain_ref, free_hbm, tgt_ref,
    loss_ref, grad_ref, fresh_hbm,
    qg, qm, lab, free, enc2, send, recv, fresh, off, inv, lg, tm, mx, sacc, pacc, ltb, coef, gacc,
    gsend, grecv, hsend, hrecv, st_p, st_z,
    ready,
    lab_sem, free_sem, q_sem, out_sem,
    qz_s, qz_r, qp_s, qp_r, d_s, d_r, f_s, f_r, sp_s, sp_r, sz_s, sz_r, gp_s, gp_r, gz_s, gz_r,
):
    y, z, x = lax.axis_index("y"), lax.axis_index("z"), lax.axis_index("x")
    core = lax.axis_index("core")
    me = (y * NZ + z) * NX + x
    plane = x * NY + y

    def z_peer(k):
        return (z + k) % NZ

    def plane_peer(k):
        return (x + k // NY) % NX, (y + k % NY) % NY

    def wait_all(ref, s, r):
        pltpu.make_async_copy(ref, ref, r).wait()
        pltpu.make_async_copy(ref, ref, s).wait()

    barrier = pltpu.get_barrier_semaphore()

    def greet_z(k):
        pl.semaphore_signal(barrier, inc=1, device_id={"z": z_peer(k)}, device_id_type=MESH)

    def greet_plane(k):
        tx, ty = plane_peer(k)
        pl.semaphore_signal(barrier, inc=1, device_id={"x": tx, "y": ty}, device_id_type=MESH)

    each(1, NZ, greet_z)
    each(1, NPLANE, greet_plane)
    pl.semaphore_signal(barrier, inc=1, device_id={"core": 1 - core}, device_id_type=MESH)

    q_copy = pltpu.make_async_copy(q_hbm, qg.at[plane, z], q_sem)
    q_copy.start()
    lab_copy = pltpu.make_async_copy(lab_hbm, lab, lab_sem)
    lab_copy.start()
    free_copy = pltpu.make_async_copy(free_hbm, free, free_sem)
    free_copy.start()

    hidden = dot(feat_ref[...], w_ref[...])
    scale = lax.rsqrt(jnp.mean(hidden * hidden, axis=1, keepdims=True) + 1e-06)
    encoded = (hidden * scale * gain_ref[...]).astype(BF16)
    enc2[0:ROWS, :] = encoded[:, 0:HALF]
    enc2[ROWS : 2 * ROWS, :] = encoded[:, HALF:D]

    q_copy.wait()
    pl.semaphore_wait(barrier, NZ - 1 + NPLANE - 1 + 1)

    def ready_z(k):
        pl.semaphore_signal(ready, inc=1, device_id={"z": z_peer(k)}, device_id_type=MESH)

    def gather_z(k):
        pltpu.make_async_remote_copy(
            qg.at[plane, z], qg.at[plane, z], qz_s, qz_r, device_id={"z": z_peer(k)}, device_id_type=MESH
        ).start()

    each(1, NZ, ready_z)
    each(1, NZ, gather_z)

    block = me * 2 + core
    row = lax.broadcasted_iota(I32, (2 * NCLS, LANES), 0)
    owner_base = (row // 2) * SLOT_ROWS
    parts = []
    inside = []
    for k in range(3):
        part = tgt_ref[pl.ds(3 * block + k, 1), :] - owner_base
        parts.append(part.astype(F32))
        inside.append((part >= 0) & (part < SLOT_ROWS))
    picks = three_of(parts, inside)
    even = row % 2 == 0
    for r in range(3):
        hit = [part == picks[r] for part in parts]
        one = [jnp.where(h & even, 1.0, 0.0).astype(BF16) for h in hit]
        two = [jnp.where(h & ~even, 1.0, 0.0).astype(BF16) for h in hit]
        chosen = dot(jnp.concatenate(one + two, axis=1), enc2[...])
        send[:, :, r * HALF : (r + 1) * HALF] = chosen.astype(BF16).reshape(NCLS, 2, HALF)

    wait_all(qg.at[plane, pl.ds(0, NZ - 1)], qz_s, qz_r)
    pl.semaphore_wait(ready, NZ - 1)

    def gather_plane(k):
        tx, ty = plane_peer(k)
        pltpu.make_async_remote_copy(
            qg.at[plane], qg.at[plane], qp_s, qp_r, device_id={"x": tx, "y": ty}, device_id_type=MESH
        ).start()

    def dispatch(k):
        tz = z_peer(k % NZ)
        tx, ty = plane_peer(k // NZ)
        dest = (ty * NZ + tz) * NX + tx
        pltpu.make_async_remote_copy(
            send.at[dest], recv.at[me], d_s, d_r, device_id={"y": ty, "z": tz, "x": tx}, device_id_type=MESH
        ).start()

    each(1, NPLANE, gather_plane)
    each(1, NCLS, dispatch)
    recv[me] = send[me]

    parts = []
    inside = []
    for k in range(3):
        first = tgt_ref[pl.ds(k, NCLS, stride=6), :]
        second = tgt_ref[pl.ds(3 + k, NCLS, stride=6), :]
        part = jnp.where(core == 0, first, second) - (me * SLOT_ROWS + core * ROWS)
        parts.append(part.astype(F32))
        inside.append((part >= 0) & (part < ROWS))
    picks = three_of(parts, inside)
    lane = lax.broadcasted_iota(I32, (NCLS, ROWS), 1).astype(F32)
    put = jnp.concatenate([jnp.where(lane == p, 1.0, 0.0).astype(BF16) for p in picks], axis=0)

    slot = slot_ref[0]
    ids = pos_ref[core]
    valid = ids >= 0
    count = jnp.sum(jnp.where(valid, 1.0, 0.0), axis=1, keepdims=True)
    inv[...] = jnp.broadcast_to(1.0 / count, (NQ, LANES))
    local = jnp.where(valid, ids - me * LABELS_DEV, -LABELS_DEV)
    for j in range(POS):
        off[j] = jnp.broadcast_to(local[:, j : j + 1], (NQ, LANES))

    def slot_of(k):
        return lax.rem(slot + 1 + k, SLOTS)

    nblocks = NQ // CHUNK

    def mass(k):
        base = slot_of(k) * SLOT_ROWS

        def rows(b):
            at = pl.ds(b * CHUNK, CHUNK)
            share = inv[at, :]
            lane_id = lax.broadcasted_iota(I32, (CHUNK, LANES), 1) + base
            offs = [off[j, at, :] - lane_id for j in range(POS)]
            for c in range(TILES):
                acc = jnp.zeros((CHUNK, LANES), F32)
                for j in range(POS):
                    acc = acc + jnp.where(offs[j] == c * LANES, share, 0.0)
                tm[k, at, c * LANES : (c + 1) * LANES] = acc

        each(0, nblocks, rows)

    each(0, SLOTS, mass)

    lab_copy.wait()
    wait_all(qg.at[pl.ds(0, NPLANE - 1)], qp_s, qp_r)
    qm[...] = qg[...].reshape(NQ, D)

    def peaks(k, values):
        lg[k] = values
        top = values[:, 0:LANES]
        for c in range(1, TILES):
            top = jnp.maximum(top, values[:, c * LANES : (c + 1) * LANES])
        return top

    def logits_of(k, peak):
        return jnp.maximum(peak, peaks(k, dot_t(qm[...], lab[slot_of(k)])))

    peak = lax.fori_loop(0, SLOTS - 1, logits_of, jnp.full((NQ, LANES), -jnp.inf, F32))
    mx[...] = jnp.broadcast_to(jnp.max(peak, axis=1, keepdims=True), (NQ, LANES))
    sacc[...] = jnp.zeros((NQ, LANES), F32)
    pacc[...] = jnp.zeros((NQ, LANES), F32)

    def sums(k):
        def rows(b):
            at = pl.ds(b * CHUNK, CHUNK)
            top = mx[at, :]
            s = sacc[at, :]
            p = pacc[at, :]
            for c in range(TILES):
                value = lg[k, at, c * LANES : (c + 1) * LANES]
                s = s + jnp.exp(value - top)
                p = p + tm[k, at, c * LANES : (c + 1) * LANES] * value
            sacc[at, :] = s
            pacc[at, :] = p

        each(0, nblocks, rows)

    each(0, SLOTS - 1, sums)

    free_copy.wait()
    wait_all(recv.at[pl.ds(0, NCLS - 1)], d_s, d_r)
    arrived = recv[...].reshape(2 * NCLS, 3 * HALF)
    pick_row = lax.broadcasted_iota(I32, (NCLS, 2 * NCLS), 0) * 2
    pick_col = lax.broadcasted_iota(I32, (NCLS, 2 * NCLS), 1)
    for c in range(2):
        take = jnp.where(pick_col == pick_row + c, 1.0, 0.0).astype(BF16)
        half = dot(take, arrived).astype(BF16)
        stacked = jnp.concatenate([half[:, r * HALF : (r + 1) * HALF] for r in range(3)], axis=0)
        placed = lax.dot_general(put, stacked, (((0,), (0,)), ((), ())), preferred_element_type=F32)
        cols = slice(c * HALF, (c + 1) * HALF)
        fresh[core, :, cols] = (free[:, cols].astype(F32) + placed).astype(BF16)
    swap = pltpu.make_async_remote_copy(
        fresh.at[core], fresh.at[core], f_s, f_r, device_id={"core": 1 - core}, device_id_type=MESH
    )
    swap.start()
    out_copy = pltpu.make_async_copy(fresh.at[core], fresh_hbm, out_sem)
    out_copy.start()
    swap.wait()
    new = fresh[...].reshape(SLOT_ROWS, D)
    peak = peaks(SLOTS - 1, dot_t(qm[...], new))
    old = mx[...]
    top = jnp.maximum(old, jnp.broadcast_to(jnp.max(peak, axis=1, keepdims=True), (NQ, LANES)))
    sacc[...] = sacc[...] * jnp.exp(old - top)
    mx[...] = top
    sums(SLOTS - 1)

    st_p[plane, 0:1, :] = mx[...].T[0:1, :]
    st_p[plane, 1:2, :] = jnp.sum(sacc[...].T, axis=0, keepdims=True)
    st_p[plane, 2:3, :] = jnp.sum(pacc[...].T, axis=0, keepdims=True)
    st_p[plane, 3:4, :] = jnp.zeros((1, NQ), F32)

    def stats_plane(k):
        tx, ty = plane_peer(k)
        pltpu.make_async_remote_copy(
            st_p.at[plane], st_p.at[plane], sp_s, sp_r, device_id={"x": tx, "y": ty}, device_id_type=MESH
        ).start()

    each(1, NPLANE, stats_plane)
    wait_all(st_p.at[pl.ds(0, NPLANE - 1)], sp_s, sp_r)
    peak, total, positive = merged(st_p, NPLANE)
    st_z[z, 0:1, :] = peak
    st_z[z, 1:2, :] = total
    st_z[z, 2:3, :] = positive
    st_z[z, 3:4, :] = jnp.zeros((1, NQ), F32)

    def stats_z(k):
        pltpu.make_async_remote_copy(
            st_z.at[z], st_z.at[z], sz_s, sz_r, device_id={"z": z_peer(k)}, device_id_type=MESH
        ).start()

    each(1, NZ, stats_z)
    wait_all(st_z.at[pl.ds(0, NZ - 1)], sz_s, sz_r)
    peak, total, positive = merged(st_z, NZ)
    log_total = peak + jnp.log(total)
    loss = log_total - positive
    own = (plane * NZ + z) * 2
    query = lax.broadcasted_iota(I32, (1, NQ), 1)
    for i in range(2):
        loss_ref[:, i : i + 1] = jnp.sum(jnp.where(query == own + i, loss, 0.0), axis=1, keepdims=True)
    ltb[...] = jnp.broadcast_to(log_total, (LANES, NQ)).T

    def coefficients(k):
        def rows(b):
            at = pl.ds(b * CHUNK, CHUNK)
            level = ltb[at, :]
            for c in range(TILES):
                cols = slice(c * LANES, (c + 1) * LANES)
                coef[k, at, cols] = (jnp.exp(lg[k, at, cols] - level) - tm[k, at, cols]).astype(BF16)

        each(0, nblocks, rows)

    each(0, SLOTS, coefficients)
    gacc[...] = dot(coef[SLOTS - 1], new)

    def gradients(k):
        gacc[...] += dot(coef[k], lab[slot_of(k)])

    each(0, SLOTS - 1, gradients)
    gsend[...] = gacc[...].astype(BF16).reshape(NPLANE, 2 * NZ, D)

    def scatter_plane(k):
        tx, ty = plane_peer(k)
        pltpu.make_async_remote_copy(
            gsend.at[tx * NY + ty], grecv.at[plane], gp_s, gp_r, device_id={"x": tx, "y": ty}, device_id_type=MESH
        ).start()

    each(1, NPLANE, scatter_plane)
    grecv[plane] = gsend[plane]
    wait_all(grecv.at[pl.ds(0, NPLANE - 1)], gp_s, gp_r)
    part = grecv[0].astype(F32)
    for i in range(1, NPLANE):
        part = part + grecv[i].astype(F32)
    hsend[...] = part.reshape(NZ, 2, D)

    def scatter_z(k):
        tz = z_peer(k)
        pltpu.make_async_remote_copy(
            hsend.at[tz], hrecv.at[z], gz_s, gz_r, device_id={"z": tz}, device_id_type=MESH
        ).start()

    each(1, NZ, scatter_z)
    hrecv[z] = hsend[z]
    wait_all(hrecv.at[pl.ds(0, NZ - 1)], gz_s, gz_r)
    whole = hrecv[0]
    for i in range(1, NZ):
        whole = whole + hrecv[i]
    grad_ref[...] = whole.astype(BF16)
    out_copy.wait()


def per_device(
    queries,
    positives,
    label_vectors,
    refresh_slot,
    features,
    encoder_weight,
    encoder_gain,
    free_vectors,
    targets,
):
    in_order = positives.reshape(2, NY, NZ, NX, 2, POS).transpose(0, 3, 1, 2, 4, 5).reshape(2, NQ, POS)
    vmem = pl.BlockSpec(memory_space=pltpu.VMEM)
    hbm = pl.BlockSpec(memory_space=pl.ANY)
    dma = pltpu.SemaphoreType.DMA
    loss, grads, refreshed = pl.pallas_call(
        kernel,
        out_shape=(
            jax.ShapeDtypeStruct((1, 2), F32),
            jax.ShapeDtypeStruct((2, D), BF16),
            jax.ShapeDtypeStruct((ROWS, D), BF16),
        ),
        in_specs=[pl.BlockSpec(memory_space=pltpu.SMEM), hbm, vmem, hbm, vmem, vmem, vmem, hbm, vmem],
        out_specs=(vmem, vmem, hbm),
        scratch_shapes=[
            pltpu.VMEM((NPLANE, NZ, 2, D), BF16),
            pltpu.VMEM((NQ, D), BF16),
            pltpu.VMEM((SLOTS, SLOT_ROWS, D), BF16),
            pltpu.VMEM((ROWS, D), BF16),
            pltpu.VMEM((2 * ROWS, HALF), BF16),
            pltpu.VMEM((NCLS, 2, 3 * HALF), BF16),
            pltpu.VMEM((NCLS, 2, 3 * HALF), BF16),
            pltpu.VMEM((2, ROWS, D), BF16),
            pltpu.VMEM((POS, NQ, LANES), I32),
            pltpu.VMEM((NQ, LANES), F32),
            pltpu.VMEM((SLOTS, NQ, SLOT_ROWS), F32),
            pltpu.VMEM((SLOTS, NQ, SLOT_ROWS), F32),
            pltpu.VMEM((NQ, LANES), F32),
            pltpu.VMEM((NQ, LANES), F32),
            pltpu.VMEM((NQ, LANES), F32),
            pltpu.VMEM((NQ, LANES), F32),
            pltpu.VMEM((SLOTS, NQ, SLOT_ROWS), BF16),
            pltpu.VMEM((NQ, D), F32),
            pltpu.VMEM((NPLANE, 2 * NZ, D), BF16),
            pltpu.VMEM((NPLANE, 2 * NZ, D), BF16),
            pltpu.VMEM((NZ, 2, D), F32),
            pltpu.VMEM((NZ, 2, D), F32),
            pltpu.VMEM((NPLANE, 4, NQ), F32),
            pltpu.VMEM((NZ, 4, NQ), F32),
            pltpu.SemaphoreType.REGULAR,
        ]
        + [dma] * 20,
        compiler_params=pltpu.CompilerParams(
            collective_id=0, has_side_effects=True, vmem_limit_bytes=60 * 2**20
        ),
    )(
        refresh_slot.reshape(1),
        queries.reshape(2, D),
        in_order,
        label_vectors.reshape(SLOTS, SLOT_ROWS, D),
        features,
        encoder_weight,
        encoder_gain.reshape(1, D),
        free_vectors,
        targets.reshape(-1, LANES),
    )
    return loss, grads.reshape(1, 2, D), refreshed


def solution(mesh):
    torus = Mesh(mesh.devices.reshape(NY, NZ, NX, mesh.shape["rep"]), CLS_REP)
    placed = (
        P("core", CLS, None),
        P(),
        P(CLS, None),
        P(),
        P(CLS_REP, None),
        P(),
        P(),
        P(CLS_REP, None),
        P(),
    )
    return jax.shard_map(
        per_device,
        mesh=torus,
        in_specs=placed,
        out_specs=(P("core", CLS), P("core", CLS, None), P(CLS_REP, None)),
        check_vma=False,
    )
```

time: 243 us -> 72.2 us (0.30)
  Pallas kernels: 0 us -> 62.7 us
  local copies, waits for them, and re-layouts: 62.9 us -> 7.25 us
  starting transfers between devices: 54 us -> 0 us
  waiting for transfers between devices: 48.7 us -> 0 us
  blocking collectives: 22.2 us -> 0 us
  matrix products: 21.1 us -> 0 us
  other arithmetic: 17 us -> 0 us
  between operations: 15.1 us -> 1.29 us
    pallas_call x0 -> x1, Pallas kernels: none -> 62.7 us  [per_device(): pl.pallas_call(kernel, out_shape=(jax.ShapeDtypeStruct((1, 2), F32), jax....]
    all_to_all x7 -> x0, starting transfers between devices: 53.9 us -> none  [the longest x5 34.1 us: copy_for_each(): lax.all_to_all(jnp.broadcast_to(shard[None], (length, *shard.shape)), axi...]
    all_to_all x7 -> x0, waiting for transfers between devices: 48.7 us -> none  [the longest x5 29.8 us: copy_for_each(): lax.all_to_all(jnp.broadcast_to(shard[None], (length, *shard.shape)), axi...]
    gather x5 -> x0, local copies, waits for them, and re-layouts: 35.3 us -> none  [the longest x3 30.9 us: per_device(): jnp.take_along_axis(logits, jnp.clip(label_offsets, 0, usable_count - 1),...]
    all_to_all x2 -> x0, blocking collectives: 22.2 us -> none  [the longest x1 11.9 us: sum_at_owner(): lax.all_to_all(pieces, axis, split_axis=0, concat_axis=0, tiled=True)]
    dot_general x3 -> x0, matrix products: 21.1 us -> none  [the longest x1 11.3 us: per_device(): jnp.dot(coefficients, current, preferred_element_type=jnp.float32)]
    sort x2 -> x0, local copies, waits for them, and re-layouts: 9.75 us -> none  [per_device(): jnp.sort(jnp.where(kept_rows, row_offsets, half_rows), axis=1)]
    sort x2 -> x0, other arithmetic: 7.54 us -> none  [the longest x1 3.77 us: per_device(): jnp.argsort(own_targets)]
  transfers between devices with their start and end apart: 8 -> 0, of which waited for: 6 -> 0; matrix products, arithmetic and copies ran while one was open for 20% -> 0% of each run, Pallas kernels for 0% -> 0%
where the time goes in v1:
time: 72.2 us; the launch traced here: 71.3 us
  Pallas kernels  62.7 us (87%)
  local copies, waits for them, and re-layouts  7.25 us (10%)
  between operations  1.29 us (2%)
    pallas_call x1, Pallas kernels, per_device(): pl.pallas_call(kernel, out_shape=(jax.ShapeDtypeStruct((1, 2), F32), jax....  62.7 us
    unnamed x4, local copies, waits for them, and re-layouts  5.18 us

profile of v1, /device:TPU:32, one launch (start us, length us, event | category | flops | bytes accessed | tf_op | source)
XLA Modules:
  0.0 71.3 jit_solution(9479709050918520251)
XLA Ops:
  1.3 1.3 %reshape.35.gain_ref = f32[1,768]{1,0:T(1,128)} reshape(f32[768]{0:T(1024)} %param.15) | data formatting | bytes 6144 | tf_op jit(solution)/shard_map/reshape | solution.py:427
  2.5 0.8 %copy.13 = s32[2,256,4]{2,1,0:T(8,128)S(1)} copy(s32[2,256,4]{1,2,0:T(4,128)} %param.10) | data formatting | bytes 16384 | tf_op args[1]
  3.4 0.8 %copy.14 = s32[2,4,4,8,2,4]{5,4,3,2,1,0:T(2,128)} copy(s32[2,4,4,8,2,4]{5,4,1,3,2,0:T(2,128)S(1)} %bitcast.12) | data formatting | bytes 16384 | tf_op jit(solution)/shard_map/transpose | solution.py:376
  4.2 62.7 %shard_map.112 = (f32[1,2]{1,0:T(1,128)}, bf16[2,768]{1,0:T(2,128)(2,1)}, bf16[384,768]{1,0:T(8,128)(2,1)}) custom-call(s32[1]{0:T(128)} %bitcast.9.slot_ref, bf16[2,768]{1,0:T(2,128)(2,1)} %bitcast.14, s32[2,256,4]{2,1,0:T(8,128)} %bitcast.11, bf16[8,768,768]{2,1,0:T(8,128)(2,1)} %bitcast.10, bf16[384,768]{1,0:T(8,128)(2,1)} %feat_ref.1, ...), custom_call_target="tpu_custom_call" | custom-call | tf_op jit(solution)/shard_map/pallas_call | solution.py:380
  67.0 1.2 %copy.19 = f32[1,2]{1,0:T(1,128)} copy(f32[1,2]{1,0:T(1,128)} %get-tuple-element.12) | data formatting | bytes 16
  68.1 1.3 %copy.20 = bf16[1,2,768]{2,1,0:T(2,128)(2,1)} copy(bf16[1,2,768]{2,1,0:T(2,128)(2,1)} %bitcast.15) | data formatting | bytes 6144
  69.4 1.9 %copy.21 = bf16[384,768]{1,0:T(8,128)(2,1)} copy(bf16[384,768]{1,0:T(8,128)(2,1)} %get-tuple-element.14) | data formatting | bytes 1179648

commit v2 on v1

--- a/solution.py
+++ b/solution.py
@@ -26,6 +26,8 @@
 CHUNK = 32
 LANES = 128
 TILES = SLOT_ROWS // LANES
+EARLY = 3
+MIDDLE = 5
 
 
 def dot(a, b):
@@ -69,12 +71,13 @@
 
 
 def kernel(
-    slot_ref, q_hbm, pos_ref, lab_hbm, feat_ref, w_ref, gain_ref, free_hbm, tgt_ref,
+    slot_ref, q_hbm, pos_hbm, lab_hbm, feat_hbm, w_hbm, gain_hbm, free_hbm, tgt_hbm,
     loss_ref, grad_ref, fresh_hbm,
-    qg, qm, lab, free, enc2, send, recv, fresh, off, inv, lg, tm, mx, sacc, pacc, ltb, coef, gacc,
+    pos_ref, feat_ref, w_ref, gain_ref, tgt_ref,
+    qg, qm, lab, free, enc2, send, recv, put, fresh, off, inv, lg, cnt, mx, top_ref, sacc, pacc, ltb, coef, gacc, gu, gt,
     gsend, grecv, hsend, hrecv, st_p, st_z,
     ready,
-    lab_sem, free_sem, q_sem, out_sem,
+    lab_sem, free_sem, q_sem, out_sem, w_sem, feat_sem, small_sem,
     qz_s, qz_r, qp_s, qp_r, d_s, d_r, f_s, f_r, sp_s, sp_r, sz_s, sz_r, gp_s, gp_r, gz_s, gz_r,
 ):
     y, z, x = lax.axis_index("y"), lax.axis_index("z"), lax.axis_index("x")
@@ -106,17 +109,26 @@
     pl.semaphore_signal(barrier, inc=1, device_id={"core": 1 - core}, device_id_type=MESH)
 
     q_copy = pltpu.make_async_copy(q_hbm, qg.at[plane, z], q_sem)
-    q_copy.start()
+    w_copy = pltpu.make_async_copy(w_hbm, w_ref, w_sem)
+    feat_copy = pltpu.make_async_copy(feat_hbm, feat_ref, feat_sem)
+    gain_copy = pltpu.make_async_copy(gain_hbm, gain_ref, small_sem.at[0])
+    pos_copy = pltpu.make_async_copy(pos_hbm, pos_ref, small_sem.at[1])
+    tgt_copy = pltpu.make_async_copy(tgt_hbm, tgt_ref, small_sem.at[2])
+    free_copy = pltpu.make_async_copy(free_hbm, free, free_sem)
     lab_copy = pltpu.make_async_copy(lab_hbm, lab, lab_sem)
-    lab_copy.start()
-    free_copy = pltpu.make_async_copy(free_hbm, free, free_sem)
-    free_copy.start()
-
+    for copy in (w_copy, feat_copy, q_copy, gain_copy, tgt_copy, pos_copy, free_copy, lab_copy):
+        copy.start()
+
+    w_copy.wait()
+    feat_copy.wait()
+    gain_copy.wait()
     hidden = dot(feat_ref[...], w_ref[...])
     scale = lax.rsqrt(jnp.mean(hidden * hidden, axis=1, keepdims=True) + 1e-06)
-    encoded = (hidden * scale * gain_ref[...]).astype(BF16)
-    enc2[0:ROWS, :] = encoded[:, 0:HALF]
-    enc2[ROWS : 2 * ROWS, :] = encoded[:, HALF:D]
+    for c in range(2):
+        for j in range(TILES // 2):
+            i = c * (TILES // 2) + j
+            cols = hidden[:, i * LANES : (i + 1) * LANES] * scale * gain_ref[i : i + 1, :]
+            enc2[c * ROWS : (c + 1) * ROWS, j * LANES : (j + 1) * LANES] = cols.astype(BF16)
 
     q_copy.wait()
     pl.semaphore_wait(barrier, NZ - 1 + NPLANE - 1 + 1)
@@ -132,6 +144,7 @@
     each(1, NZ, ready_z)
     each(1, NZ, gather_z)
 
+    tgt_copy.wait()
     block = me * 2 + core
     row = lax.broadcasted_iota(I32, (2 * NCLS, LANES), 0)
     owner_base = (row // 2) * SLOT_ROWS
@@ -181,14 +194,28 @@
         inside.append((part >= 0) & (part < ROWS))
     picks = three_of(parts, inside)
     lane = lax.broadcasted_iota(I32, (NCLS, ROWS), 1).astype(F32)
-    put = jnp.concatenate([jnp.where(lane == p, 1.0, 0.0).astype(BF16) for p in picks], axis=0)
-
+    spread_row = lax.broadcasted_iota(I32, (NCLS, 2 * NCLS), 0) * 2
+    spread_col = lax.broadcasted_iota(I32, (NCLS, 2 * NCLS), 1)
+    for r in range(3):
+        to_row = jnp.where(lane == picks[r], 1.0, 0.0).T.astype(BF16)
+        for c in range(2):
+            spread = jnp.where(spread_col == spread_row + c, 1.0, 0.0).astype(BF16)
+            put[c, :, r * 2 * NCLS : (r + 1) * 2 * NCLS] = dot(to_row, spread).astype(BF16)
+
+    pos_copy.wait()
     slot = slot_ref[0]
-    ids = pos_ref[core]
-    valid = ids >= 0
+    q_row = lax.broadcasted_iota(I32, (NQ, NQ), 0)
+    q_col = lax.broadcasted_iota(I32, (NQ, NQ), 1)
+    natural = ((((q_row // 16) % NY) * NZ + (q_row // 2) % NZ) * NX + q_row // 64) * 2 + q_row % 2
+    order = jnp.where(q_col == natural, 1.0, 0.0).astype(BF16)
+    ids = pos_ref[core] + 1
+    ids = sum(
+        dot_t(order, ((ids >> (8 * i)) & 255).astype(F32).astype(BF16)) * float(256**i) for i in range(3)
+    )
+    valid = ids >= 1.0
     count = jnp.sum(jnp.where(valid, 1.0, 0.0), axis=1, keepdims=True)
     inv[...] = jnp.broadcast_to(1.0 / count, (NQ, LANES))
-    local = jnp.where(valid, ids - me * LABELS_DEV, -LABELS_DEV)
+    local = jnp.where(valid, ids.astype(I32) - (1 + me * LABELS_DEV), -LABELS_DEV)
     for j in range(POS):
         off[j] = jnp.broadcast_to(local[:, j : j + 1], (NQ, LANES))
 
@@ -197,90 +224,109 @@
 
     nblocks = NQ // CHUNK
 
-    def mass(k):
+    def counts(k):
         base = slot_of(k) * SLOT_ROWS
 
         def rows(b):
             at = pl.ds(b * CHUNK, CHUNK)
-            share = inv[at, :]
             lane_id = lax.broadcasted_iota(I32, (CHUNK, LANES), 1) + base
             offs = [off[j, at, :] - lane_id for j in range(POS)]
             for c in range(TILES):
                 acc = jnp.zeros((CHUNK, LANES), F32)
                 for j in range(POS):
-                    acc = acc + jnp.where(offs[j] == c * LANES, share, 0.0)
-                tm[k, at, c * LANES : (c + 1) * LANES] = acc
+                    acc = acc + jnp.where(offs[j] == c * LANES, 1.0, 0.0)
+                cnt[k, at, c * LANES : (c + 1) * LANES] = acc.astype(BF16)
 
         each(0, nblocks, rows)
 
-    each(0, SLOTS, mass)
+    each(0, SLOTS, counts)
 
     lab_copy.wait()
     wait_all(qg.at[pl.ds(0, NPLANE - 1)], qp_s, qp_r)
     qm[...] = qg[...].reshape(NQ, D)
 
-    def peaks(k, values):
-        lg[k] = values
+    def highest(values):
         top = values[:, 0:LANES]
-        for c in range(1, TILES):
+        for c in range(1, values.shape[1] // LANES):
             top = jnp.maximum(top, values[:, c * LANES : (c + 1) * LANES])
         return top
 
     def logits_of(k, peak):
-        return jnp.maximum(peak, peaks(k, dot_t(qm[...], lab[slot_of(k)])))
+        values = dot_t(qm[...], lab[slot_of(k)])
+        lg[k] = values
+        return jnp.maximum(peak, highest(values))
 
     peak = lax.fori_loop(0, SLOTS - 1, logits_of, jnp.full((NQ, LANES), -jnp.inf, F32))
     mx[...] = jnp.broadcast_to(jnp.max(peak, axis=1, keepdims=True), (NQ, LANES))
     sacc[...] = jnp.zeros((NQ, LANES), F32)
     pacc[...] = jnp.zeros((NQ, LANES), F32)
 
-    def sums(k):
+    def weights(k, level_ref):
         def rows(b):
             at = pl.ds(b * CHUNK, CHUNK)
-            top = mx[at, :]
+            low_at = pl.ds(NQ + b * CHUNK, CHUNK)
+            level = level_ref[at, :]
             s = sacc[at, :]
             p = pacc[at, :]
             for c in range(TILES):
-                value = lg[k, at, c * LANES : (c + 1) * LANES]
-                s = s + jnp.exp(value - top)
-                p = p + tm[k, at, c * LANES : (c + 1) * LANES] * value
+                cols = slice(c * LANES, (c + 1) * LANES)
+                value = lg[k, at, cols]
+                many = cnt[k, at, cols].astype(F32)
+                e = jnp.exp(value - level)
+                s = s + e
+                p = p + many * value
+                high = e.astype(BF16)
+                coef[k, at, cols] = high
+                coef[k, low_at, cols] = jnp.where(many > 0.0, e - high.astype(F32), 0.0).astype(BF16)
             sacc[at, :] = s
             pacc[at, :] = p
 
         each(0, nblocks, rows)
 
-    each(0, SLOTS - 1, sums)
+    each(0, SLOTS - 1, lambda k: weights(k, mx))
+    gacc[...] = jnp.zeros((3 * NQ, D), F32)
+
+    def gradients(k):
+        vectors = lab[slot_of(k)]
+        gacc[0 : 2 * NQ, :] += dot(coef[k], vectors)
+        gacc[2 * NQ : 3 * NQ, :] += dot(cnt[k], vectors)
+
+    each(0, EARLY, gradients)
 
     free_copy.wait()
     wait_all(recv.at[pl.ds(0, NCLS - 1)], d_s, d_r)
     arrived = recv[...].reshape(2 * NCLS, 3 * HALF)
-    pick_row = lax.broadcasted_iota(I32, (NCLS, 2 * NCLS), 0) * 2
-    pick_col = lax.broadcasted_iota(I32, (NCLS, 2 * NCLS), 1)
-    for c in range(2):
-        take = jnp.where(pick_col == pick_row + c, 1.0, 0.0).astype(BF16)
-        half = dot(take, arrived).astype(BF16)
-        stacked = jnp.concatenate([half[:, r * HALF : (r + 1) * HALF] for r in range(3)], axis=0)
-        placed = lax.dot_general(put, stacked, (((0,), (0,)), ((), ())), preferred_element_type=F32)
-        cols = slice(c * HALF, (c + 1) * HALF)
-        fresh[core, :, cols] = (free[:, cols].astype(F32) + placed).astype(BF16)
-    swap = pltpu.make_async_remote_copy(
-        fresh.at[core], fresh.at[core], f_s, f_r, device_id={"core": 1 - core}, device_id_type=MESH
-    )
-    swap.start()
+    stacked = jnp.concatenate([arrived[:, r * HALF : (r + 1) * HALF] for r in range(3)], axis=0)
+    swaps = []
+    for h in range(2):
+        at = slice(h * (ROWS // 2), (h + 1) * (ROWS // 2))
+        for c in range(2):
+            cols = slice(c * HALF, (c + 1) * HALF)
+            fresh[core, at, cols] = (free[at, cols].astype(F32) + dot(put[c, at, :], stacked)).astype(BF16)
+        swap = pltpu.make_async_remote_copy(
+            fresh.at[core, at], fresh.at[core, at], f_s.at[h], f_r.at[h],
+            device_id={"core": 1 - core}, device_id_type=MESH,
+        )
+        swap.start()
+        swaps.append(swap)
     out_copy = pltpu.make_async_copy(fresh.at[core], fresh_hbm, out_sem)
     out_copy.start()
-    swap.wait()
-    new = fresh[...].reshape(SLOT_ROWS, D)
-    peak = peaks(SLOTS - 1, dot_t(qm[...], new))
+    own_logits = dot_t(qm[...], fresh[core])
+    for swap in swaps:
+        swap.wait()
+    other_logits = dot_t(qm[...], fresh[1 - core])
+    peak = jnp.maximum(highest(own_logits), highest(other_logits))
+    lg[SLOTS - 1, :, 0:ROWS] = jnp.where(core == 0, own_logits, other_logits)
+    lg[SLOTS - 1, :, ROWS : 2 * ROWS] = jnp.where(core == 0, other_logits, own_logits)
     old = mx[...]
     top = jnp.maximum(old, jnp.broadcast_to(jnp.max(peak, axis=1, keepdims=True), (NQ, LANES)))
     sacc[...] = sacc[...] * jnp.exp(old - top)
-    mx[...] = top
-    sums(SLOTS - 1)
-
-    st_p[plane, 0:1, :] = mx[...].T[0:1, :]
+    top_ref[...] = top
+    weights(SLOTS - 1, top_ref)
+
+    st_p[plane, 0:1, :] = top_ref[...].T[0:1, :]
     st_p[plane, 1:2, :] = jnp.sum(sacc[...].T, axis=0, keepdims=True)
-    st_p[plane, 2:3, :] = jnp.sum(pacc[...].T, axis=0, keepdims=True)
+    st_p[plane, 2:3, :] = jnp.sum((pacc[...] * inv[...]).T, axis=0, keepdims=True)
     st_p[plane, 3:4, :] = jnp.zeros((1, NQ), F32)
 
     def stats_plane(k):
@@ -290,6 +336,7 @@
         ).start()
 
     each(1, NPLANE, stats_plane)
+    each(EARLY, MIDDLE, gradients)
     wait_all(st_p.at[pl.ds(0, NPLANE - 1)], sp_s, sp_r)
     peak, total, positive = merged(st_p, NPLANE)
     st_z[z, 0:1, :] = peak
@@ -303,43 +350,36 @@
         ).start()
 
     each(1, NZ, stats_z)
+    each(MIDDLE, SLOTS - 1, gradients)
+    new = fresh[...].reshape(SLOT_ROWS, D)
+    last = dot(coef[SLOTS - 1], new)
+    last_count = dot(cnt[SLOTS - 1], new)
+    factor = jnp.exp(mx[...] - top_ref[...])
+    for c in range(TILES):
+        cols = slice(c * LANES, (c + 1) * LANES)
+        gu[:, cols] = (gacc[0:NQ, cols] + gacc[NQ : 2 * NQ, cols]) * factor + (last[0:NQ, cols] + last[NQ : 2 * NQ, cols])
+        gt[:, cols] = (gacc[2 * NQ : 3 * NQ, cols] + last_count[:, cols]) * inv[...]
     wait_all(st_z.at[pl.ds(0, NZ - 1)], sz_s, sz_r)
     peak, total, positive = merged(st_z, NZ)
     log_total = peak + jnp.log(total)
+    ltb[...] = jnp.exp(top_ref[...] - jnp.broadcast_to(log_total, (LANES, NQ)).T)
+    for c in range(TILES):
+        cols = slice(c * LANES, (c + 1) * LANES)
+        gsend[:, :, cols] = (gu[:, cols] * ltb[...] - gt[:, cols]).astype(BF16).reshape(NPLANE, 2 * NZ, LANES)
+
+    def scatter_plane(k):
+        tx, ty = plane_peer(k)
+        pltpu.make_async_remote_copy(
+            gsend.at[tx * NY + ty], grecv.at[plane], gp_s, gp_r, device_id={"x": tx, "y": ty}, device_id_type=MESH
+        ).start()
+
+    each(1, NPLANE, scatter_plane)
+    grecv[plane] = gsend[plane]
     loss = log_total - positive
     own = (plane * NZ + z) * 2
     query = lax.broadcasted_iota(I32, (1, NQ), 1)
     for i in range(2):
         loss_ref[:, i : i + 1] = jnp.sum(jnp.where(query == own + i, loss, 0.0), axis=1, keepdims=True)
-    ltb[...] = jnp.broadcast_to(log_total, (LANES, NQ)).T
-
-    def coefficients(k):
-        def rows(b):
-            at = pl.ds(b * CHUNK, CHUNK)
-            level = ltb[at, :]
-            for c in range(TILES):
-                cols = slice(c * LANES, (c + 1) * LANES)
-                coef[k, at, cols] = (jnp.exp(lg[k, at, cols] - level) - tm[k, at, cols]).astype(BF16)
-
-        each(0, nblocks, rows)
-
-    each(0, SLOTS, coefficients)
-    gacc[...] = dot(coef[SLOTS - 1], new)
-
-    def gradients(k):
-        gacc[...] += dot(coef[k], lab[slot_of(k)])
-
-    each(0, SLOTS - 1, gradients)
-    gsend[...] = gacc[...].astype(BF16).reshape(NPLANE, 2 * NZ, D)
-
-    def scatter_plane(k):
-        tx, ty = plane_peer(k)
-        pltpu.make_async_remote_copy(
-            gsend.at[tx * NY + ty], grecv.at[plane], gp_s, gp_r, device_id={"x": tx, "y": ty}, device_id_type=MESH
-        ).start()
-
-    each(1, NPLANE, scatter_plane)
-    grecv[plane] = gsend[plane]
     wait_all(grecv.at[pl.ds(0, NPLANE - 1)], gp_s, gp_r)
     part = grecv[0].astype(F32)
     for i in range(1, NPLANE):
@@ -354,12 +394,32 @@
 
     each(1, NZ, scatter_z)
     hrecv[z] = hsend[z]
+    out_copy.wait()
     wait_all(hrecv.at[pl.ds(0, NZ - 1)], gz_s, gz_r)
     whole = hrecv[0]
     for i in range(1, NZ):
         whole = whole + hrecv[i]
     grad_ref[...] = whole.astype(BF16)
-    out_copy.wait()
+
+
+def hand_over(loss_in, grad_in, fresh_in, loss_out, grad_out, fresh_out, held, sems):
+    parts = 4
+    size = ROWS // parts
+
+    def piece(i):
+        return pl.ds(i * size, size)
+
+    ins = [pltpu.make_async_copy(fresh_in.at[piece(i)], held.at[piece(i)], sems.at[0, i]) for i in range(parts)]
+    outs = [pltpu.make_async_copy(held.at[piece(i)], fresh_out.at[piece(i)], sems.at[1, i]) for i in range(parts)]
+    for copy in ins:
+        copy.start()
+    loss_out[...] = loss_in[...]
+    grad_out[...] = grad_in[...]
+    for i in range(parts):
+        ins[i].wait()
+        outs[i].start()
+    for copy in outs:
+        copy.wait()
 
 
 def per_device(
@@ -373,20 +433,25 @@
     free_vectors,
     targets,
 ):
-    in_order = positives.reshape(2, NY, NZ, NX, 2, POS).transpose(0, 3, 1, 2, 4, 5).reshape(2, NQ, POS)
     vmem = pl.BlockSpec(memory_space=pltpu.VMEM)
     hbm = pl.BlockSpec(memory_space=pl.ANY)
     dma = pltpu.SemaphoreType.DMA
-    loss, grads, refreshed = pl.pallas_call(
+    results = (
+        jax.ShapeDtypeStruct((1, 2), F32),
+        jax.ShapeDtypeStruct((2, D), BF16),
+        jax.ShapeDtypeStruct((ROWS, D), BF16),
+    )
+    made = pl.pallas_call(
         kernel,
-        out_shape=(
-            jax.ShapeDtypeStruct((1, 2), F32),
-            jax.ShapeDtypeStruct((2, D), BF16),
-            jax.ShapeDtypeStruct((ROWS, D), BF16),
-        ),
-        in_specs=[pl.BlockSpec(memory_space=pltpu.SMEM), hbm, vmem, hbm, vmem, vmem, vmem, hbm, vmem],
+        out_shape=results,
+        in_specs=[pl.BlockSpec(memory_space=pltpu.SMEM)] + [hbm] * 8,
         out_specs=(vmem, vmem, hbm),
         scratch_shapes=[
+            pltpu.VMEM((2, POS, NQ), I32),
+            pltpu.VMEM((ROWS, D), BF16),
+            pltpu.VMEM((D, D), BF16),
+            pltpu.VMEM((TILES, LANES), F32),
+            pltpu.VMEM((2 * NCLS * 3, LANES), I32),
             pltpu.VMEM((NPLANE, NZ, 2, D), BF16),
             pltpu.VMEM((NQ, D), BF16),
             pltpu.VMEM((SLOTS, SLOT_ROWS, D), BF16),
@@ -394,16 +459,20 @@
             pltpu.VMEM((2 * ROWS, HALF), BF16),
             pltpu.VMEM((NCLS, 2, 3 * HALF), BF16),
             pltpu.VMEM((NCLS, 2, 3 * HALF), BF16),
+            pltpu.VMEM((2, ROWS, 3 * 2 * NCLS), BF16),
             pltpu.VMEM((2, ROWS, D), BF16),
             pltpu.VMEM((POS, NQ, LANES), I32),
             pltpu.VMEM((NQ, LANES), F32),
             pltpu.VMEM((SLOTS, NQ, SLOT_ROWS), F32),
-            pltpu.VMEM((SLOTS, NQ, SLOT_ROWS), F32),
+            pltpu.VMEM((SLOTS, NQ, SLOT_ROWS), BF16),
             pltpu.VMEM((NQ, LANES), F32),
             pltpu.VMEM((NQ, LANES), F32),
             pltpu.VMEM((NQ, LANES), F32),
             pltpu.VMEM((NQ, LANES), F32),
-            pltpu.VMEM((SLOTS, NQ, SLOT_ROWS), BF16),
+            pltpu.VMEM((NQ, LANES), F32),
+            pltpu.VMEM((SLOTS, 2 * NQ, SLOT_ROWS), BF16),
+            pltpu.VMEM((3 * NQ, D), F32),
+            pltpu.VMEM((NQ, D), F32),
             pltpu.VMEM((NQ, D), F32),
             pltpu.VMEM((NPLANE, 2 * NZ, D), BF16),
             pltpu.VMEM((NPLANE, 2 * NZ, D), BF16),
@@ -413,21 +482,32 @@
             pltpu.VMEM((NZ, 4, NQ), F32),
             pltpu.SemaphoreType.REGULAR,
         ]
-        + [dma] * 20,
+        + [dma] * 6
+        + [dma((3,))]
+        + [dma] * 6
+        + [dma((2,))] * 2
+        + [dma] * 8,
         compiler_params=pltpu.CompilerParams(
-            collective_id=0, has_side_effects=True, vmem_limit_bytes=60 * 2**20
+            collective_id=0, has_side_effects=True, vmem_limit_bytes=56 * 2**20
         ),
     )(
         refresh_slot.reshape(1),
         queries.reshape(2, D),
-        in_order,
+        jnp.swapaxes(positives, 1, 2),
         label_vectors.reshape(SLOTS, SLOT_ROWS, D),
         features,
         encoder_weight,
-        encoder_gain.reshape(1, D),
+        encoder_gain.reshape(TILES, LANES),
         free_vectors,
         targets.reshape(-1, LANES),
     )
+    loss, grads, refreshed = pl.pallas_call(
+        hand_over,
+        out_shape=results,
+        in_specs=[vmem, vmem, hbm],
+        out_specs=(vmem, vmem, hbm),
+        scratch_shapes=[pltpu.VMEM((ROWS, D), BF16), dma((2, 4))],
+    )(*made)
     return loss, grads.reshape(1, 2, D), refreshed
 
 

time: 72.2 us -> 64.8 us (0.90)
  local copies, waits for them, and re-layouts: 7.25 us -> 0 us
    unnamed x4 -> x0, local copies, waits for them, and re-layouts: 5.18 us -> none
    reshape x1 -> x0, local copies, waits for them, and re-layouts: 1.27 us -> none  [per_device(): encoder_gain.reshape(1, D)]
    transpose x1 -> x0, local copies, waits for them, and re-layouts: 0.81 us -> none  [per_device(): positives.reshape(2, NY, NZ, NX, 2, POS).transpose(0, 3, 1, 2, 4, 5)]
    pallas_call x1 -> x2, Pallas kernels: 62.7 us -> 62.8 us  [the longest x1 59.7 us: per_device(): pl.pallas_call(kernel, out_shape=results, in_specs=[pl.BlockSpec(memory_s...]
where the time goes in v2:
time: 64.8 us; the launch traced here: 64.1 us
  Pallas kernels  62.8 us (97%)
  between operations  1.29 us (2%)
    pallas_call x1, Pallas kernels, per_device(): pl.pallas_call(kernel, out_shape=results, in_specs=[pl.BlockSpec(memory_s...  59.7 us
    pallas_call x1, Pallas kernels, per_device(): pl.pallas_call(hand_over, out_shape=results, in_specs=[vmem, vmem, hbm],...  3.11 us

profile of v2, /device:TPU:32, one launch (start us, length us, event | category | flops | bytes accessed | tf_op | source)
XLA Modules:
  0.0 64.1 jit_solution(12709483257869297816)
XLA Ops:
  1.3 59.7 %shard_map.112 = (f32[1,2]{1,0:T(1,128)}, bf16[2,768]{1,0:T(2,128)(2,1)}, bf16[384,768]{1,0:T(8,128)(2,1)}) custom-call(s32[1]{0:T(128)} %bitcast.7.slot_ref, bf16[2,768]{1,0:T(2,128)(2,1)} %bitcast.12, s32[2,4,256]{2,1,0:T(4,128)} %bitcast.10, bf16[8,768,768]{2,1,0:T(8,128)(2,1)} %bitcast.8, bf16[384,768]{1,0:T(8,128)(2,1)} %feat_hbm.1, ...), custom_call_target="tpu_custom_call" | custom-call | tf_op jit(solution)/shard_map/pallas_call | solution.py:444
  61.0 3.1 %shard_map.113 = (f32[1,2]{1,0:T(1,128)}, bf16[2,768]{1,0:T(2,128)(2,1)}, bf16[384,768]{1,0:T(8,128)(2,1)}) custom-call(f32[1,2]{1,0:T(1,128)} %get-tuple-element.9.loss_in, bf16[2,768]{1,0:T(2,128)(2,1)} %get-tuple-element.10.grad_in, bf16[384,768]{1,0:T(8,128)(2,1)} %get-tuple-element.11.fresh_in), custom_call_target="tpu_custom_call" | custom-call | tf_op jit(solution)/shard_map/pallas_call | solution.py:504

commit v3 on v2

--- a/solution.py
+++ b/solution.py
@@ -26,7 +26,9 @@
 CHUNK = 32
 LANES = 128
 TILES = SLOT_ROWS // LANES
-EARLY = 3
+EARLY = 2
+UNDER_SWAP = 3
+FIRST = 21
 MIDDLE = 5
 
 
@@ -71,10 +73,10 @@
 
 
 def kernel(
-    slot_ref, q_hbm, pos_hbm, lab_hbm, feat_hbm, w_hbm, gain_hbm, free_hbm, tgt_hbm,
+    slot_hbm, q_hbm, pos_hbm, lab_hbm, feat_hbm, w_hbm, gain_hbm, free_hbm, tgt_hbm,
     loss_ref, grad_ref, fresh_hbm,
-    pos_ref, feat_ref, w_ref, gain_ref, tgt_ref,
-    qg, qm, lab, free, enc2, send, recv, put, fresh, off, inv, lg, cnt, mx, top_ref, sacc, pacc, ltb, coef, gacc, gu, gt,
+    slot_ref, pos_ref, feat_ref, w_ref, gain_ref, tgt_ref,
+    qg, qm, lab, free, enc2, send, recv, put, fresh, off, inv, lg, cnt, mx, top_ref, sacc, pacc, ltb, coef, gacc, gcnt, gu, gt,
     gsend, grecv, hsend, hrecv, st_p, st_z,
     ready,
     lab_sem, free_sem, q_sem, out_sem, w_sem, feat_sem, small_sem,
@@ -116,7 +118,8 @@
     tgt_copy = pltpu.make_async_copy(tgt_hbm, tgt_ref, small_sem.at[2])
     free_copy = pltpu.make_async_copy(free_hbm, free, free_sem)
     lab_copy = pltpu.make_async_copy(lab_hbm, lab, lab_sem)
-    for copy in (w_copy, feat_copy, q_copy, gain_copy, tgt_copy, pos_copy, free_copy, lab_copy):
+    slot_copy = pltpu.make_async_copy(slot_hbm, slot_ref, small_sem.at[3])
+    for copy in (w_copy, feat_copy, gain_copy, tgt_copy, q_copy, pos_copy, slot_copy, free_copy, lab_copy):
         copy.start()
 
     w_copy.wait()
@@ -129,20 +132,6 @@
             i = c * (TILES // 2) + j
             cols = hidden[:, i * LANES : (i + 1) * LANES] * scale * gain_ref[i : i + 1, :]
             enc2[c * ROWS : (c + 1) * ROWS, j * LANES : (j + 1) * LANES] = cols.astype(BF16)
-
-    q_copy.wait()
-    pl.semaphore_wait(barrier, NZ - 1 + NPLANE - 1 + 1)
-
-    def ready_z(k):
-        pl.semaphore_signal(ready, inc=1, device_id={"z": z_peer(k)}, device_id_type=MESH)
-
-    def gather_z(k):
-        pltpu.make_async_remote_copy(
-            qg.at[plane, z], qg.at[plane, z], qz_s, qz_r, device_id={"z": z_peer(k)}, device_id_type=MESH
-        ).start()
-
-    each(1, NZ, ready_z)
-    each(1, NZ, gather_z)
 
     tgt_copy.wait()
     block = me * 2 + core
@@ -163,8 +152,19 @@
         chosen = dot(jnp.concatenate(one + two, axis=1), enc2[...])
         send[:, :, r * HALF : (r + 1) * HALF] = chosen.astype(BF16).reshape(NCLS, 2, HALF)
 
-    wait_all(qg.at[plane, pl.ds(0, NZ - 1)], qz_s, qz_r)
-    pl.semaphore_wait(ready, NZ - 1)
+    q_copy.wait()
+    pl.semaphore_wait(barrier, NZ - 1 + NPLANE - 1 + 1)
+
+    def ready_z(k):
+        pl.semaphore_signal(ready, inc=1, device_id={"z": z_peer(k)}, device_id_type=MESH)
+
+    def gather_z(k):
+        pltpu.make_async_remote_copy(
+            qg.at[plane, z], qg.at[plane, z], qz_s, qz_r, device_id={"z": z_peer(k)}, device_id_type=MESH
+        ).start()
+
+    each(1, NZ, ready_z)
+    each(1, NZ, gather_z)
 
     def gather_plane(k):
         tx, ty = plane_peer(k)
@@ -172,16 +172,25 @@
             qg.at[plane], qg.at[plane], qp_s, qp_r, device_id={"x": tx, "y": ty}, device_id_type=MESH
         ).start()
 
-    def dispatch(k):
-        tz = z_peer(k % NZ)
-        tx, ty = plane_peer(k // NZ)
+    def dispatch(dz, j):
+        tz = z_peer(dz)
+        tx, ty = plane_peer(j)
         dest = (ty * NZ + tz) * NX + tx
         pltpu.make_async_remote_copy(
             send.at[dest], recv.at[me], d_s, d_r, device_id={"y": ty, "z": tz, "x": tx}, device_id_type=MESH
         ).start()
 
+    def dispatch_far(k):
+        dispatch(1 + k % (NZ - 1), 1 + k // (NZ - 1))
+
+    each(1, NZ, lambda k: dispatch(k, 0))
+    each(1, NPLANE, lambda j: dispatch(0, j))
+    pl.semaphore_wait(ready, NZ - 1)
+    far = (NZ - 1) * (NPLANE - 1)
+    each(0, FIRST, dispatch_far)
+    wait_all(qg.at[plane, pl.ds(0, NZ - 1)], qz_s, qz_r)
     each(1, NPLANE, gather_plane)
-    each(1, NCLS, dispatch)
+    each(FIRST, far, dispatch_far)
     recv[me] = send[me]
 
     parts = []
@@ -203,6 +212,7 @@
             put[c, :, r * 2 * NCLS : (r + 1) * 2 * NCLS] = dot(to_row, spread).astype(BF16)
 
     pos_copy.wait()
+    slot_copy.wait()
     slot = slot_ref[0]
     q_row = lax.broadcasted_iota(I32, (NQ, NQ), 0)
     q_col = lax.broadcasted_iota(I32, (NQ, NQ), 1)
@@ -242,6 +252,12 @@
     each(0, SLOTS, counts)
 
     lab_copy.wait()
+    gcnt[...] = dot(cnt[0], lab[slot_of(0)])
+
+    def count_rows(k):
+        gcnt[...] += dot(cnt[k], lab[slot_of(k)])
+
+    each(1, SLOTS - 1, count_rows)
     wait_all(qg.at[pl.ds(0, NPLANE - 1)], qp_s, qp_r)
     qm[...] = qg[...].reshape(NQ, D)
 
@@ -259,7 +275,11 @@
     peak = lax.fori_loop(0, SLOTS - 1, logits_of, jnp.full((NQ, LANES), -jnp.inf, F32))
     mx[...] = jnp.broadcast_to(jnp.max(peak, axis=1, keepdims=True), (NQ, LANES))
     sacc[...] = jnp.zeros((NQ, LANES), F32)
-    pacc[...] = jnp.zeros((NQ, LANES), F32)
+    positive = jnp.zeros((NQ, LANES), F32)
+    for c in range(TILES):
+        cols = slice(c * LANES, (c + 1) * LANES)
+        positive = positive + qm[:, cols].astype(F32) * gcnt[:, cols]
+    pacc[...] = positive
 
     def weights(k, level_ref):
         def rows(b):
@@ -267,31 +287,24 @@
             low_at = pl.ds(NQ + b * CHUNK, CHUNK)
             level = level_ref[at, :]
             s = sacc[at, :]
-            p = pacc[at, :]
             for c in range(TILES):
                 cols = slice(c * LANES, (c + 1) * LANES)
-                value = lg[k, at, cols]
-                many = cnt[k, at, cols].astype(F32)
-                e = jnp.exp(value - level)
+                e = jnp.exp(lg[k, at, cols] - level)
                 s = s + e
-                p = p + many * value
                 high = e.astype(BF16)
                 coef[k, at, cols] = high
-                coef[k, low_at, cols] = jnp.where(many > 0.0, e - high.astype(F32), 0.0).astype(BF16)
+                coef[k, low_at, cols] = (e - high.astype(F32)).astype(BF16)
             sacc[at, :] = s
-            pacc[at, :] = p
 
         each(0, nblocks, rows)
 
     each(0, SLOTS - 1, lambda k: weights(k, mx))
-    gacc[...] = jnp.zeros((3 * NQ, D), F32)
+    gacc[...] = dot(coef[0], lab[slot_of(0)])
 
     def gradients(k):
-        vectors = lab[slot_of(k)]
-        gacc[0 : 2 * NQ, :] += dot(coef[k], vectors)
-        gacc[2 * NQ : 3 * NQ, :] += dot(cnt[k], vectors)
-
-    each(0, EARLY, gradients)
+        gacc[...] += dot(coef[k], lab[slot_of(k)])
+
+    each(1, EARLY, gradients)
 
     free_copy.wait()
     wait_all(recv.at[pl.ds(0, NCLS - 1)], d_s, d_r)
@@ -312,6 +325,7 @@
     out_copy = pltpu.make_async_copy(fresh.at[core], fresh_hbm, out_sem)
     out_copy.start()
     own_logits = dot_t(qm[...], fresh[core])
+    each(EARLY, UNDER_SWAP, gradients)
     for swap in swaps:
         swap.wait()
     other_logits = dot_t(qm[...], fresh[1 - core])
@@ -323,6 +337,11 @@
     sacc[...] = sacc[...] * jnp.exp(old - top)
     top_ref[...] = top
     weights(SLOTS - 1, top_ref)
+    positive = pacc[...]
+    for c in range(TILES):
+        cols = slice(c * LANES, (c + 1) * LANES)
+        positive = positive + cnt[SLOTS - 1, :, cols].astype(F32) * lg[SLOTS - 1, :, cols]
+    pacc[...] = positive
 
     st_p[plane, 0:1, :] = top_ref[...].T[0:1, :]
     st_p[plane, 1:2, :] = jnp.sum(sacc[...].T, axis=0, keepdims=True)
@@ -336,7 +355,7 @@
         ).start()
 
     each(1, NPLANE, stats_plane)
-    each(EARLY, MIDDLE, gradients)
+    each(UNDER_SWAP, MIDDLE, gradients)
     wait_all(st_p.at[pl.ds(0, NPLANE - 1)], sp_s, sp_r)
     peak, total, positive = merged(st_p, NPLANE)
     st_z[z, 0:1, :] = peak
@@ -358,7 +377,7 @@
     for c in range(TILES):
         cols = slice(c * LANES, (c + 1) * LANES)
         gu[:, cols] = (gacc[0:NQ, cols] + gacc[NQ : 2 * NQ, cols]) * factor + (last[0:NQ, cols] + last[NQ : 2 * NQ, cols])
-        gt[:, cols] = (gacc[2 * NQ : 3 * NQ, cols] + last_count[:, cols]) * inv[...]
+        gt[:, cols] = (gcnt[:, cols] + last_count[:, cols]) * inv[...]
     wait_all(st_z.at[pl.ds(0, NZ - 1)], sz_s, sz_r)
     peak, total, positive = merged(st_z, NZ)
     log_total = peak + jnp.log(total)
@@ -402,20 +421,18 @@
     grad_ref[...] = whole.astype(BF16)
 
 
-def hand_over(loss_in, grad_in, fresh_in, loss_out, grad_out, fresh_out, held, sems):
-    parts = 4
+def hand_over(loss_in, grad_in, fresh_in, loss_out, grad_out, fresh_out, loss, grad, fresh, sems):
+    parts = 2
     size = ROWS // parts
-
-    def piece(i):
-        return pl.ds(i * size, size)
-
-    ins = [pltpu.make_async_copy(fresh_in.at[piece(i)], held.at[piece(i)], sems.at[0, i]) for i in range(parts)]
-    outs = [pltpu.make_async_copy(held.at[piece(i)], fresh_out.at[piece(i)], sems.at[1, i]) for i in range(parts)]
+    moves = [(loss_in, loss, loss_out), (grad_in, grad, grad_out)]
+    for i in range(parts):
+        at = pl.ds(i * size, size)
+        moves.append((fresh_in.at[at], fresh.at[at], fresh_out.at[at]))
+    ins = [pltpu.make_async_copy(a, b, sems.at[0, i]) for i, (a, b, _) in enumerate(moves)]
+    outs = [pltpu.make_async_copy(b, c, sems.at[1, i]) for i, (_, b, c) in enumerate(moves)]
     for copy in ins:
         copy.start()
-    loss_out[...] = loss_in[...]
-    grad_out[...] = grad_in[...]
-    for i in range(parts):
+    for i in range(len(moves)):
         ins[i].wait()
         outs[i].start()
     for copy in outs:
@@ -444,9 +461,10 @@
     made = pl.pallas_call(
         kernel,
         out_shape=results,
-        in_specs=[pl.BlockSpec(memory_space=pltpu.SMEM)] + [hbm] * 8,
+        in_specs=[hbm] * 9,
         out_specs=(vmem, vmem, hbm),
         scratch_shapes=[
+            pltpu.SMEM((1,), I32),
             pltpu.VMEM((2, POS, NQ), I32),
             pltpu.VMEM((ROWS, D), BF16),
             pltpu.VMEM((D, D), BF16),
@@ -471,7 +489,8 @@
             pltpu.VMEM((NQ, LANES), F32),
             pltpu.VMEM((NQ, LANES), F32),
             pltpu.VMEM((SLOTS, 2 * NQ, SLOT_ROWS), BF16),
-            pltpu.VMEM((3 * NQ, D), F32),
+            pltpu.VMEM((2 * NQ, D), F32),
+            pltpu.VMEM((NQ, D), F32),
             pltpu.VMEM((NQ, D), F32),
             pltpu.VMEM((NQ, D), F32),
             pltpu.VMEM((NPLANE, 2 * NZ, D), BF16),
@@ -483,7 +502,7 @@
             pltpu.SemaphoreType.REGULAR,
         ]
         + [dma] * 6
-        + [dma((3,))]
+        + [dma((4,))]
         + [dma] * 6
         + [dma((2,))] * 2
         + [dma] * 8,
@@ -504,9 +523,14 @@
     loss, grads, refreshed = pl.pallas_call(
         hand_over,
         out_shape=results,
-        in_specs=[vmem, vmem, hbm],
-        out_specs=(vmem, vmem, hbm),
-        scratch_shapes=[pltpu.VMEM((ROWS, D), BF16), dma((2, 4))],
+        in_specs=[hbm] * 3,
+        out_specs=(hbm,) * 3,
+        scratch_shapes=[
+            pltpu.VMEM((1, 2), F32),
+            pltpu.VMEM((2, D), BF16),
+            pltpu.VMEM((ROWS, D), BF16),
+            dma((2, 4)),
+        ],
     )(*made)
     return loss, grads.reshape(1, 2, D), refreshed
 

time: 64.8 us -> 64.5 us (level)
  no operation moved by 1% of the time
where the time goes in v3:
time: 64.5 us; the launch traced here: 64 us
  Pallas kernels  62.7 us (97%)
  between operations  1.29 us (2%)
    pallas_call x1, Pallas kernels, per_device(): pl.pallas_call(kernel, out_shape=results, in_specs=[hbm] * 9, out_specs=(...  60.8 us
    pallas_call x1, Pallas kernels, per_device(): pl.pallas_call(hand_over, out_shape=results, in_specs=[hbm] * 3, out_spec...  1.85 us

profile of v3, /device:TPU:32, one launch (start us, length us, event | category | flops | bytes accessed | tf_op | source)
XLA Modules:
  0.0 64.0 jit_solution(11038240999744382130)
XLA Ops:
  1.3 60.8 %shard_map.112 = (f32[1,2]{1,0:T(1,128)}, bf16[2,768]{1,0:T(2,128)(2,1)}, bf16[384,768]{1,0:T(8,128)(2,1)}) custom-call(s32[1]{0:T(128)} %bitcast.7.slot_hbm, bf16[2,768]{1,0:T(2,128)(2,1)} %bitcast.12, s32[2,4,256]{2,1,0:T(4,128)} %bitcast.10, bf16[8,768,768]{2,1,0:T(8,128)(2,1)} %bitcast.8, bf16[384,768]{1,0:T(8,128)(2,1)} %feat_hbm.1, ...), custom_call_target="tpu_custom_call" | custom-call | tf_op jit(solution)/shard_map/pallas_call | solution.py:461
  62.1 1.9 %shard_map.113 = (f32[1,2]{1,0:T(1,128)}, bf16[2,768]{1,0:T(2,128)(2,1)}, bf16[384,768]{1,0:T(8,128)(2,1)}) custom-call(f32[1,2]{1,0:T(1,128)} %get-tuple-element.9.loss_in, bf16[2,768]{1,0:T(2,128)(2,1)} %get-tuple-element.10.grad_in, bf16[384,768]{1,0:T(8,128)(2,1)} %get-tuple-element.11.fresh_in), custom_call_target="tpu_custom_call" | custom-call | tf_op jit(solution)/shard_map/pallas_call | solution.py:523

commit v4 on v3

--- a/solution.py
+++ b/solution.py
@@ -28,7 +28,7 @@
 TILES = SLOT_ROWS // LANES
 EARLY = 2
 UNDER_SWAP = 3
-FIRST = 21
+FIRST = 4
 MIDDLE = 5
 
 
@@ -88,10 +88,10 @@
     plane = x * NY + y
 
     def z_peer(k):
-        return (z + k) % NZ
+        return lax.rem(z + k, NZ)
 
     def plane_peer(k):
-        return (x + k // NY) % NX, (y + k % NY) % NY
+        return lax.rem(x + lax.div(k, NY), NX), lax.rem(y + lax.rem(k, NY), NY)
 
     def wait_all(ref, s, r):
         pltpu.make_async_copy(ref, ref, r).wait()
@@ -180,18 +180,17 @@
             send.at[dest], recv.at[me], d_s, d_r, device_id={"y": ty, "z": tz, "x": tx}, device_id_type=MESH
         ).start()
 
-    def dispatch_far(k):
-        dispatch(1 + k % (NZ - 1), 1 + k // (NZ - 1))
+    def dispatch_far(j):
+        tx, ty = plane_peer(j)
+        for dz in range(1, NZ):
+            tz = z_peer(dz)
+            dest = (ty * NZ + tz) * NX + tx
+            pltpu.make_async_remote_copy(
+                send.at[dest], recv.at[me], d_s, d_r, device_id={"y": ty, "z": tz, "x": tx}, device_id_type=MESH
+            ).start()
 
     each(1, NZ, lambda k: dispatch(k, 0))
     each(1, NPLANE, lambda j: dispatch(0, j))
-    pl.semaphore_wait(ready, NZ - 1)
-    far = (NZ - 1) * (NPLANE - 1)
-    each(0, FIRST, dispatch_far)
-    wait_all(qg.at[plane, pl.ds(0, NZ - 1)], qz_s, qz_r)
-    each(1, NPLANE, gather_plane)
-    each(FIRST, far, dispatch_far)
-    recv[me] = send[me]
 
     parts = []
     inside = []
@@ -250,6 +249,13 @@
         each(0, nblocks, rows)
 
     each(0, SLOTS, counts)
+
+    pl.semaphore_wait(ready, NZ - 1)
+    each(1, FIRST, dispatch_far)
+    wait_all(qg.at[plane, pl.ds(0, NZ - 1)], qz_s, qz_r)
+    each(1, NPLANE, gather_plane)
+    each(FIRST, NPLANE, dispatch_far)
+    recv[me] = send[me]
 
     lab_copy.wait()
     gcnt[...] = dot(cnt[0], lab[slot_of(0)])

time: 64.5 us -> 64.8 us (level)
  Pallas kernels: 62.7 us -> 63.4 us
    pallas_call x1, Pallas kernels: 60.8 us -> 61.5 us  [per_device(): pl.pallas_call(kernel, out_shape=results, in_specs=[hbm] * 9, out_specs=(...]
where the time goes in v4:
time: 64.8 us; the launch traced here: 64.7 us
  Pallas kernels  63.4 us (98%)
  between operations  1.29 us (2%)
    pallas_call x1, Pallas kernels, per_device(): pl.pallas_call(kernel, out_shape=results, in_specs=[hbm] * 9, out_specs=(...  61.5 us
    pallas_call x1, Pallas kernels, per_device(): pl.pallas_call(hand_over, out_shape=results, in_specs=[hbm] * 3, out_spec...  1.85 us

profile of v4, /device:TPU:32, one launch (start us, length us, event | category | flops | bytes accessed | tf_op | source)
XLA Modules:
  0.0 64.7 jit_solution(16008399711348059011)
XLA Ops:
  1.3 61.5 %shard_map.112 = (f32[1,2]{1,0:T(1,128)}, bf16[2,768]{1,0:T(2,128)(2,1)}, bf16[384,768]{1,0:T(8,128)(2,1)}) custom-call(s32[1]{0:T(128)} %bitcast.7.slot_hbm, bf16[2,768]{1,0:T(2,128)(2,1)} %bitcast.12, s32[2,4,256]{2,1,0:T(4,128)} %bitcast.10, bf16[8,768,768]{2,1,0:T(8,128)(2,1)} %bitcast.8, bf16[384,768]{1,0:T(8,128)(2,1)} %feat_hbm.1, ...), custom_call_target="tpu_custom_call" | custom-call | tf_op jit(solution)/shard_map/pallas_call | solution.py:467
  62.8 1.9 %shard_map.113 = (f32[1,2]{1,0:T(1,128)}, bf16[2,768]{1,0:T(2,128)(2,1)}, bf16[384,768]{1,0:T(8,128)(2,1)}) custom-call(f32[1,2]{1,0:T(1,128)} %get-tuple-element.9.loss_in, bf16[2,768]{1,0:T(2,128)(2,1)} %get-tuple-element.10.grad_in, bf16[384,768]{1,0:T(8,128)(2,1)} %get-tuple-element.11.fresh_in), custom_call_target="tpu_custom_call" | custom-call | tf_op jit(solution)/shard_map/pallas_call | solution.py:529

commit v5 on v4

--- a/solution.py
+++ b/solution.py
@@ -26,9 +26,9 @@
 CHUNK = 32
 LANES = 128
 TILES = SLOT_ROWS // LANES
-EARLY = 2
-UNDER_SWAP = 3
-FIRST = 4
+EARLY = 1
+UNDER_SWAP = 1
+FIRST = 1
 MIDDLE = 5
 
 
@@ -93,9 +93,11 @@
     def plane_peer(k):
         return lax.rem(x + lax.div(k, NY), NX), lax.rem(y + lax.rem(k, NY), NY)
 
+    sent = []
+
     def wait_all(ref, s, r):
         pltpu.make_async_copy(ref, ref, r).wait()
-        pltpu.make_async_copy(ref, ref, s).wait()
+        sent.append((ref, s))
 
     barrier = pltpu.get_barrier_semaphore()
 
@@ -189,8 +191,6 @@
                 send.at[dest], recv.at[me], d_s, d_r, device_id={"y": ty, "z": tz, "x": tx}, device_id_type=MESH
             ).start()
 
-    each(1, NZ, lambda k: dispatch(k, 0))
-    each(1, NPLANE, lambda j: dispatch(0, j))
 
     parts = []
     inside = []
@@ -254,6 +254,8 @@
     each(1, FIRST, dispatch_far)
     wait_all(qg.at[plane, pl.ds(0, NZ - 1)], qz_s, qz_r)
     each(1, NPLANE, gather_plane)
+    each(1, NZ, lambda k: dispatch(k, 0))
+    each(1, NPLANE, lambda j: dispatch(0, j))
     each(FIRST, NPLANE, dispatch_far)
     recv[me] = send[me]
 
@@ -305,7 +307,6 @@
         each(0, nblocks, rows)
 
     each(0, SLOTS - 1, lambda k: weights(k, mx))
-    gacc[...] = dot(coef[0], lab[slot_of(0)])
 
     def gradients(k):
         gacc[...] += dot(coef[k], lab[slot_of(k)])
@@ -332,8 +333,9 @@
     out_copy.start()
     own_logits = dot_t(qm[...], fresh[core])
     each(EARLY, UNDER_SWAP, gradients)
-    for swap in swaps:
-        swap.wait()
+    for h, swap in enumerate(swaps):
+        swap.wait_recv()
+        sent.append((fresh.at[0, pl.ds(0, ROWS // 2)], f_s.at[h]))
     other_logits = dot_t(qm[...], fresh[1 - core])
     peak = jnp.maximum(highest(own_logits), highest(other_logits))
     lg[SLOTS - 1, :, 0:ROWS] = jnp.where(core == 0, own_logits, other_logits)
@@ -361,6 +363,7 @@
         ).start()
 
     each(1, NPLANE, stats_plane)
+    gacc[...] = dot(coef[0], lab[slot_of(0)])
     each(UNDER_SWAP, MIDDLE, gradients)
     wait_all(st_p.at[pl.ds(0, NPLANE - 1)], sp_s, sp_r)
     peak, total, positive = merged(st_p, NPLANE)
@@ -425,6 +428,8 @@
     for i in range(1, NZ):
         whole = whole + hrecv[i]
     grad_ref[...] = whole.astype(BF16)
+    for ref, s in sent:
+        pltpu.make_async_copy(ref, ref, s).wait()
 
 
 def hand_over(loss_in, grad_in, fresh_in, loss_out, grad_out, fresh_out, loss, grad, fresh, sems):

time: 64.8 us -> 61.7 us (0.952); the launches traced: 64.7 us -> 60.9 us
  Pallas kernels: 63.4 us -> 59.6 us
    pallas_call x1, Pallas kernels: 61.5 us -> 57.8 us  [per_device(): pl.pallas_call(kernel, out_shape=results, in_specs=[hbm] * 9, out_specs=(...]
where the time goes in v5:
time: 61.7 us; the launch traced here: 60.9 us
  Pallas kernels  59.6 us (97%)
  between operations  1.29 us (2%)
    pallas_call x1, Pallas kernels, per_device(): pl.pallas_call(kernel, out_shape=results, in_specs=[hbm] * 9, out_specs=(...  57.8 us
    pallas_call x1, Pallas kernels, per_device(): pl.pallas_call(hand_over, out_shape=results, in_specs=[hbm] * 3, out_spec...  1.85 us

profile of v5, /device:TPU:32, one launch (start us, length us, event | category | flops | bytes accessed | tf_op | source)
XLA Modules:
  0.0 60.9 jit_solution(6302971564110590026)
XLA Ops:
  1.3 57.8 %shard_map.112 = (f32[1,2]{1,0:T(1,128)}, bf16[2,768]{1,0:T(2,128)(2,1)}, bf16[384,768]{1,0:T(8,128)(2,1)}) custom-call(s32[1]{0:T(128)} %bitcast.7.slot_hbm, bf16[2,768]{1,0:T(2,128)(2,1)} %bitcast.12, s32[2,4,256]{2,1,0:T(4,128)} %bitcast.10, bf16[8,768,768]{2,1,0:T(8,128)(2,1)} %bitcast.8, bf16[384,768]{1,0:T(8,128)(2,1)} %feat_hbm.1, ...), custom_call_target="tpu_custom_call" | custom-call | tf_op jit(solution)/shard_map/pallas_call | solution.py:472
  59.1 1.9 %shard_map.113 = (f32[1,2]{1,0:T(1,128)}, bf16[2,768]{1,0:T(2,128)(2,1)}, bf16[384,768]{1,0:T(8,128)(2,1)}) custom-call(f32[1,2]{1,0:T(1,128)} %get-tuple-element.9.loss_in, bf16[2,768]{1,0:T(2,128)(2,1)} %get-tuple-element.10.grad_in, bf16[384,768]{1,0:T(8,128)(2,1)} %get-tuple-element.11.fresh_in), custom_call_target="tpu_custom_call" | custom-call | tf_op jit(solution)/shard_map/pallas_call | solution.py:534

commit v6 on v5

--- a/solution.py
+++ b/solution.py
@@ -26,8 +26,6 @@
 CHUNK = 32
 LANES = 128
 TILES = SLOT_ROWS // LANES
-EARLY = 1
-UNDER_SWAP = 1
 FIRST = 1
 MIDDLE = 5
 
@@ -311,7 +309,6 @@
     def gradients(k):
         gacc[...] += dot(coef[k], lab[slot_of(k)])
 
-    each(1, EARLY, gradients)
 
     free_copy.wait()
     wait_all(recv.at[pl.ds(0, NCLS - 1)], d_s, d_r)
@@ -332,7 +329,7 @@
     out_copy = pltpu.make_async_copy(fresh.at[core], fresh_hbm, out_sem)
     out_copy.start()
     own_logits = dot_t(qm[...], fresh[core])
-    each(EARLY, UNDER_SWAP, gradients)
+    gacc[...] = dot(coef[0], lab[slot_of(0)])
     for h, swap in enumerate(swaps):
         swap.wait_recv()
         sent.append((fresh.at[0, pl.ds(0, ROWS // 2)], f_s.at[h]))
@@ -363,8 +360,7 @@
         ).start()
 
     each(1, NPLANE, stats_plane)
-    gacc[...] = dot(coef[0], lab[slot_of(0)])
-    each(UNDER_SWAP, MIDDLE, gradients)
+    each(1, MIDDLE, gradients)
     wait_all(st_p.at[pl.ds(0, NPLANE - 1)], sp_s, sp_r)
     peak, total, positive = merged(st_p, NPLANE)
     st_z[z, 0:1, :] = peak

time: 61.7 us -> 61.2 us (level)
  no operation moved by 1% of the time
where the time goes in v6:
time: 61.2 us; the launch traced here: 60.5 us
  Pallas kernels  59.2 us (97%)
  between operations  1.29 us (2%)
    pallas_call x1, Pallas kernels, per_device(): pl.pallas_call(kernel, out_shape=results, in_specs=[hbm] * 9, out_specs=(...  57.4 us
    pallas_call x1, Pallas kernels, per_device(): pl.pallas_call(hand_over, out_shape=results, in_specs=[hbm] * 3, out_spec...  1.85 us

profile of v6, /device:TPU:32, one launch (start us, length us, event | category | flops | bytes accessed | tf_op | source)
XLA Modules:
  0.0 60.5 jit_solution(16915177074387152462)
XLA Ops:
  1.3 57.4 %shard_map.112 = (f32[1,2]{1,0:T(1,128)}, bf16[2,768]{1,0:T(2,128)(2,1)}, bf16[384,768]{1,0:T(8,128)(2,1)}) custom-call(s32[1]{0:T(128)} %bitcast.7.slot_hbm, bf16[2,768]{1,0:T(2,128)(2,1)} %bitcast.12, s32[2,4,256]{2,1,0:T(4,128)} %bitcast.10, bf16[8,768,768]{2,1,0:T(8,128)(2,1)} %bitcast.8, bf16[384,768]{1,0:T(8,128)(2,1)} %feat_hbm.1, ...), custom_call_target="tpu_custom_call" | custom-call | tf_op jit(solution)/shard_map/pallas_call | solution.py:468
  58.7 1.9 %shard_map.113 = (f32[1,2]{1,0:T(1,128)}, bf16[2,768]{1,0:T(2,128)(2,1)}, bf16[384,768]{1,0:T(8,128)(2,1)}) custom-call(f32[1,2]{1,0:T(1,128)} %get-tuple-element.9.loss_in, bf16[2,768]{1,0:T(2,128)(2,1)} %get-tuple-element.10.grad_in, bf16[384,768]{1,0:T(8,128)(2,1)} %get-tuple-element.11.fresh_in), custom_call_target="tpu_custom_call" | custom-call | tf_op jit(solution)/shard_map/pallas_call | solution.py:530
